TPU v7x, 32 devices: a whole 2x2x4 slice. The times are simulated.
32 devices in a mesh: dp: 8 (over z, x), mp: 4 (over y, core).
Axes of the slice: x: 2, y: 2, z: 4, core: 2. Of those that a mesh axis runs over, the one named last changes fastest.
Arguments:
- inputs: float32 [8, 1024, 1536], P('dp', 'mp'), may hold values from -6 to 6
- segments: int32 [8, 1024], P('dp'), may hold values from 0 to 7, never falling along the last dimension, each value on 1 to 512 neighbouring positions
- attend_gain: float32 [1536], P(('dp', 'mp')), may hold values from 0.1 to 1.9
- feed_gain: float32 [1536], P(('dp', 'mp')), may hold values from 0.1 to 1.9
- w_query: float32 [1536, 768], P('dp', 'mp'), may hold values from -0.01953125 to 0.01953125
- w_key: float32 [1536, 768], P('dp', 'mp'), may hold values from -0.15625 to 0.15625
- w_value: float32 [1536, 768], P('dp', 'mp'), may hold values from -0.15625 to 0.15625
- w_mixer: float32 [768, 1536], P('mp', 'dp'), may hold values from -0.875 to 0.875
- rel_table: float32 [32, 12], P(None, 'mp'), may hold values from -4 to 4
- w_gate: float32 [1536, 3968], P('dp', 'mp'), may hold values from -0.15625 to 0.15625
- w_lift: float32 [1536, 3968], P('dp', 'mp'), may hold values from -0.15625 to 0.15625
- w_down: float32 [3968, 1536], P('mp', 'dp'), may hold values from -0.09375 to 0.09375
- cotangent: float32 [8, 1024, 1536], P('dp', 'mp'), may hold values from -6 to 6
Outputs:
- output: float32 [8, 1024, 1536], P('dp', 'mp')
- input_grad: float32 [8, 1024, 1536], P('dp', 'mp')
- attend_grad: float32 [1536], P(('dp', 'mp'))
- feed_grad: float32 [1536], P(('dp', 'mp'))
- query_grad: float32 [1536, 768], P('dp', 'mp')
- key_grad: float32 [1536, 768], P('dp', 'mp')
- value_grad: float32 [1536, 768], P('dp', 'mp')
- mixer_grad: float32 [768, 1536], P('mp', 'dp')
- table_grad: float32 [32, 12], P(None, 'mp')
- gate_grad: float32 [1536, 3968], P('dp', 'mp')
- lift_grad: float32 [1536, 3968], P('dp', 'mp')
- down_grad: float32 [3968, 1536], P('mp', 'dp')
Inputs may be any that keep to these rules, and one draw needn't show every extreme that they name: `segments`: in each row the segment ids never fall, and each id covers between 1 and 512 consecutive positions; one covers exactly 512.
All inputs are finite; a program needn't handle non-finite values.
Results may differ from a plain program's by a relative error of at most 0.013.
The roundings to bfloat16 on the way count: a program that leaves them out, or rounds other values in their place, can miss the bound.
Values may be sent and summed in bfloat16 or wider, within the bound.
A program may use at most 192 MiB of HBM per device.

v0:
```python
import jax
import jax.numpy as jnp
from jax import lax
from jax.sharding import PartitionSpec as P

EPSILON = 1e-06
THRESHOLDS = (8, 12, 16, 23, 32, 46, 64, 91)
HIGHEST = lax.Precision.HIGHEST
MASKED = -1e30


def bucket_table(length):
    places = jnp.arange(length, dtype=jnp.int32)
    offset = places[None, :] - places[:, None]
    distance = jnp.abs(offset)
    far_bucket = 7 + sum(((distance >= limit).astype(jnp.int32) for limit in THRESHOLDS))
    near = jnp.where(distance < 8, distance, far_bucket)
    return near + jnp.where(offset > 0, 16, 0).astype(jnp.int32)


def scaled_norm(values, gain):
    return values * lax.rsqrt(jnp.mean(values * values, axis=-1, keepdims=True) + EPSILON) * gain


def gated(gate, lift):
    return jax.nn.gelu(gate, approximate=True) * lift


def dense(left, weight):
    return jnp.einsum("rld,de->rle", left, weight, preferred_element_type=jnp.float32)


def dense_back(grad, weight):
    return jnp.einsum("rle,de->rld", grad, weight, preferred_element_type=jnp.float32)


def weight_term(left, grad):
    return jnp.einsum("rld,rle->de", left, grad, preferred_element_type=jnp.float32)


def collect(part):
    return lax.all_gather(part, "mp", axis=1, tiled=True)


def spread(part):
    return lax.psum_scatter(part, "mp", scatter_dimension=1, tiled=True)


def split_heads(rows, count):
    return rows.reshape(rows.shape[0], count, rows.shape[1] // count)


def bias_blocks(table_part, buckets):
    length = buckets.shape[0]
    block = min(length, 128)
    tiles = buckets.reshape(length // block, block, length)
    codes = jnp.arange(table_part.shape[0], dtype=jnp.int32)

    def bias_one_block(tile):
        onehot = (tile[None] == codes[:, None, None]).astype(jnp.float32)
        return jnp.einsum("bij,bh->hij", onehot, table_part, precision=HIGHEST)

    pieces = lax.map(bias_one_block, tiles)
    return jnp.transpose(pieces, (1, 0, 2, 3)).reshape(table_part.shape[1], length, length)


def table_terms(score_total, buckets, count):
    heads_here, length, _ = score_total.shape
    block = min(length, 128)
    tiles = buckets.reshape(length // block, block, length)
    pieces = jnp.transpose(
        score_total.reshape(heads_here, length // block, block, length), (1, 0, 2, 3)
    )
    codes = jnp.arange(count, dtype=jnp.int32)

    def table_one_block(total, pair):
        tile, piece = pair
        onehot = (tile[None] == codes[:, None, None]).astype(jnp.float32)
        return (total + jnp.einsum("bij,hij->bh", onehot, piece, precision=HIGHEST), None)

    result, _ = lax.scan(
        table_one_block, jnp.zeros((count, heads_here), jnp.float32), (tiles, pieces)
    )
    return result


def local(
    inputs,
    segments,
    attend_gain,
    feed_gain,
    w_query,
    w_key,
    w_value,
    w_mixer,
    rel_table,
    w_gate,
    w_lift,
    w_down,
    cotangent,
):
    length = segments.shape[1]
    heads_here = rel_table.shape[1]
    buckets = bucket_table(length)
    bias = bias_blocks(rel_table, buckets)
    gains = (
        lax.all_gather(attend_gain.astype(jnp.bfloat16), ("dp", "mp"), axis=0, tiled=True),
        lax.all_gather(feed_gain.astype(jnp.bfloat16), ("dp", "mp"), axis=0, tiled=True),
    )
    first_gain = gains[0].astype(jnp.float32)
    second_gain = gains[1].astype(jnp.float32)
    attention_full = (
        lax.all_gather(w_query.astype(jnp.bfloat16), "dp", axis=0, tiled=True),
        lax.all_gather(w_key.astype(jnp.bfloat16), "dp", axis=0, tiled=True),
        lax.all_gather(w_value.astype(jnp.bfloat16), "dp", axis=0, tiled=True),
        lax.all_gather(w_mixer.astype(jnp.bfloat16), "dp", axis=1, tiled=True),
    )
    feed_full = (
        lax.all_gather(w_gate.astype(jnp.bfloat16), "dp", axis=0, tiled=True),
        lax.all_gather(w_lift.astype(jnp.bfloat16), "dp", axis=0, tiled=True),
        lax.all_gather(w_down.astype(jnp.bfloat16), "dp", axis=1, tiled=True),
    )

    def score_rows(query_heads, key_heads, segment_row):
        scores = (
            jnp.einsum("ihe,jhe->hij", query_heads, key_heads, preferred_element_type=jnp.float32)
            + bias
        )
        same = segment_row[:, None] == segment_row[None, :]
        return jnp.where(same[None], scores, MASKED)

    normed = scaled_norm(inputs, first_gain).astype(jnp.bfloat16)
    normed_full = collect(normed)
    query = dense(normed_full, attention_full[0]).astype(jnp.bfloat16)
    keys = dense(normed_full, attention_full[1]).astype(jnp.bfloat16)
    values = dense(normed_full, attention_full[2]).astype(jnp.bfloat16)

    def attend(row):
        query_row, key_row, value_row, segment_row = row
        query_heads = split_heads(query_row, heads_here)
        key_heads = split_heads(key_row, heads_here)
        value_heads = split_heads(value_row, heads_here)
        scores = score_rows(query_heads, key_heads, segment_row)
        largest = jnp.max(scores, axis=-1, keepdims=True)
        raised = jnp.exp(scores - largest)
        totals = jnp.sum(raised, axis=-1, keepdims=True)
        probs = (raised / totals).astype(jnp.bfloat16)
        context = jnp.einsum("hij,jhe->ihe", probs, value_heads, preferred_element_type=jnp.float32)
        return (
            context.astype(jnp.bfloat16).reshape(length, -1),
            (largest + jnp.log(totals))[..., 0],
        )

    context, logsum = lax.map(attend, (query, keys, values, segments))
    middle = inputs + spread(dense(context, attention_full[3]))
    normed_two = scaled_norm(middle, second_gain).astype(jnp.bfloat16)
    second_full = collect(normed_two)
    gate = dense(second_full, feed_full[0])
    lift = dense(second_full, feed_full[1])
    hidden = gated(gate, lift).astype(jnp.bfloat16)
    output = middle + spread(dense(hidden, feed_full[2]))
    feed_back = (
        lax.all_gather(w_gate.astype(jnp.bfloat16), "dp", axis=0, tiled=True),
        lax.all_gather(w_lift.astype(jnp.bfloat16), "dp", axis=0, tiled=True),
        lax.all_gather(w_down.astype(jnp.bfloat16), "dp", axis=1, tiled=True),
    )
    down_full = collect(cotangent.astype(jnp.bfloat16))
    hidden_cot = dense_back(down_full, feed_back[2])
    down_term = weight_term(hidden, down_full)
    _, gated_pull = jax.vjp(gated, gate, lift)
    gate_cot, lift_cot = gated_pull(hidden_cot)
    gate_cot = gate_cot.astype(jnp.bfloat16)
    lift_cot = lift_cot.astype(jnp.bfloat16)
    gate_term = weight_term(second_full, gate_cot)
    lift_term = weight_term(second_full, lift_cot)
    second_cot = spread(dense_back(gate_cot, feed_back[0]) + dense_back(lift_cot, feed_back[1]))
    _, second_pull = jax.vjp(scaled_norm, middle, second_gain)
    middle_from_norm, second_gain_term = second_pull(second_cot)
    middle_cot = cotangent + middle_from_norm
    attention_back = (
        lax.all_gather(w_query.astype(jnp.bfloat16), "dp", axis=0, tiled=True),
        lax.all_gather(w_key.astype(jnp.bfloat16), "dp", axis=0, tiled=True),
        lax.all_gather(w_value.astype(jnp.bfloat16), "dp", axis=0, tiled=True),
        lax.all_gather(w_mixer.astype(jnp.bfloat16), "dp", axis=1, tiled=True),
    )
    mixed_full = collect(middle_cot.astype(jnp.bfloat16))
    context_cot = dense_back(mixed_full, attention_back[3]).astype(jnp.bfloat16)
    mixer_term = weight_term(context, mixed_full)

    def attend_back(total, row):
        query_row, key_row, value_row, segment_row, log_row, cot_row = row
        query_heads = split_heads(query_row, heads_here)
        key_heads = split_heads(key_row, heads_here)
        value_heads = split_heads(value_row, heads_here)
        cot_heads = split_heads(cot_row, heads_here)
        scores = score_rows(query_heads, key_heads, segment_row)
        probs = jnp.exp(scores - log_row[:, :, None])
        value_cot = jnp.einsum(
            "hij,ihe->jhe",
            probs.astype(jnp.bfloat16),
            cot_heads,
            preferred_element_type=jnp.float32,
        )
        prob_cot = jnp.einsum(
            "ihe,jhe->hij", cot_heads, value_heads, preferred_element_type=jnp.float32
        )
        inner = jnp.sum(probs * prob_cot, axis=-1, keepdims=True)
        score_cot = (probs * (prob_cot - inner)).astype(jnp.bfloat16)
        query_cot = jnp.einsum(
            "hij,jhe->ihe", score_cot, key_heads, preferred_element_type=jnp.float32
        )
        key_cot = jnp.einsum(
            "hij,ihe->jhe", score_cot, query_heads, preferred_element_type=jnp.float32
        )
        outputs = (
            query_cot.astype(jnp.bfloat16).reshape(length, -1),
            key_cot.astype(jnp.bfloat16).reshape(length, -1),
            value_cot.astype(jnp.bfloat16).reshape(length, -1),
        )
        return (total + score_cot.astype(jnp.float32), outputs)

    score_total, cots = lax.scan(
        attend_back,
        jnp.zeros((heads_here, length, length), jnp.float32),
        (query, keys, values, segments, logsum, context_cot),
    )
    query_cot, key_cot, value_cot = cots
    query_term = weight_term(normed_full, query_cot)
    key_term = weight_term(normed_full, key_cot)
    value_term = weight_term(normed_full, value_cot)
    first_cot = spread(
        dense_back(query_cot, attention_back[0])
        + dense_back(key_cot, attention_back[1])
        + dense_back(value_cot, attention_back[2])
    )
    _, first_pull = jax.vjp(scaled_norm, inputs, first_gain)
    input_from_norm, first_gain_term = first_pull(first_cot)
    input_grad = middle_cot + input_from_norm
    table_grad = lax.psum(table_terms(score_total, buckets, rel_table.shape[0]), "dp")
    gain_grads = (
        lax.psum_scatter(first_gain_term, ("dp", "mp"), scatter_dimension=0, tiled=True),
        lax.psum_scatter(second_gain_term, ("dp", "mp"), scatter_dimension=0, tiled=True),
    )
    summed = (
        lax.psum_scatter(query_term, "dp", scatter_dimension=0, tiled=True),
        lax.psum_scatter(key_term, "dp", scatter_dimension=0, tiled=True),
        lax.psum_scatter(value_term, "dp", scatter_dimension=0, tiled=True),
        lax.psum_scatter(mixer_term, "dp", scatter_dimension=1, tiled=True),
        lax.psum_scatter(gate_term, "dp", scatter_dimension=0, tiled=True),
        lax.psum_scatter(lift_term, "dp", scatter_dimension=0, tiled=True),
        lax.psum_scatter(down_term, "dp", scatter_dimension=1, tiled=True),
    )
    return (
        output,
        input_grad,
        gain_grads[0],
        gain_grads[1],
        summed[0],
        summed[1],
        summed[2],
        summed[3],
        table_grad,
        summed[4],
        summed[5],
        summed[6],
    )


def solution(mesh):
    return jax.shard_map(
        local,
        mesh=mesh,
        in_specs=(
            P("dp", "mp", None),
            P("dp", None),
            P(("dp", "mp")),
            P(("dp", "mp")),
            P("dp", "mp"),
            P("dp", "mp"),
            P("dp", "mp"),
            P("mp", "dp"),
            P(None, "mp"),
            P("dp", "mp"),
            P("dp", "mp"),
            P("mp", "dp"),
            P("dp", "mp", None),
        ),
        out_specs=(
            P("dp", "mp", None),
            P("dp", "mp", None),
            P(("dp", "mp")),
            P(("dp", "mp")),
            P("dp", "mp"),
            P("dp", "mp"),
            P("dp", "mp"),
            P("mp", "dp"),
            P(None, "mp"),
            P("dp", "mp"),
            P("dp", "mp"),
            P("mp", "dp"),
        ),
        check_vma=False,
    )
```

profile of v0, /device:TPU:0, one launch (start us, length us, event | category | flops | bytes accessed | tf_op | source)
XLA Modules:
  0.0 1423.3 jit_solution(14468035993226204309)
XLA Ops:
  9.8 42.1 %all-reduce.5 = (bf16[1536]{0:T(1024)(128)(2,1)S(1)}, bf16[1536]{0:T(1024)(128)(2,1)S(1)}) all-reduce(bf16[1536]{0:T(1024)(128)(2,1)S(1)} %dynamic-update-slice, bf16[1536]{0:T(1024)(128)(2,1)S(1)} %dynamic-update-slice.1), channel_id=1, replica_groups=mesh['dp'=8,'mp'=4] {'dp','mp'}, use_global_device_ids=true, to_apply=%add | all-reduce | flops 3072 | bytes 12288
  57.2 6.1 fusion.25
  63.4 59.5 %while.6 = (s32[]{:T(128)}, f32[8,3,128,1024]{3,1,2,0:T(4,128)}, s32[8,128,1024]{2,1,0:T(8,128)}, f32[32,3]{0,1:T(4,128)S(1)}, s32[]{:T(128)}) while((s32[]{:T(128)}, f32[8,3,128,1024]{3,1,2,0:T(4,128)}, s32[8,128,1024]{2,1,0:T(8,128)}, f32[32,3]{0,1:T(4,128)S(1)}, s32[]{:T(128)}) %tuple.99), condition=%wide.region_2.3_spmd.clone, body=%wide.region_1.2_spmd.clone.sunk | while | flops 155189248 | bytes 3670977 | solution.py:63
  64.5 6.3 bitcast_dynamic-update-slice_fusion.2
  71.9 6.3 bitcast_dynamic-update-slice_fusion.2
  79.3 6.4 bitcast_dynamic-update-slice_fusion.2
  86.7 6.3 bitcast_dynamic-update-slice_fusion.2
  94.1 6.3 bitcast_dynamic-update-slice_fusion.2
  101.5 6.2 bitcast_dynamic-update-slice_fusion.2
  108.8 6.3 bitcast_dynamic-update-slice_fusion.2
  116.2 6.2 bitcast_dynamic-update-slice_fusion.2
  122.9 17.6 %copy.27 = f32[3,8,128,1024]{3,2,1,0:T(8,128)} copy(f32[3,8,128,1024]{3,0,2,1:T(4,128)} %bitcast.157) | data formatting | bytes 25165824 | tf_op jit(solution)/shard_map/transpose | solution.py:64
  140.7 32.3 %all_gather.49 = bf16[1536,192]{1,0:T(8,128)(2,1)S(1)} all-gather(bf16[192,192]{1,0:T(8,128)(2,1)S(1)} %convert_element_type.177), channel_id=1, replica_groups=mesh['dp'=8,'mp'=4] {'dp'}, dimensions={0}, use_global_device_ids=true | all-gather | bytes 663552 | tf_op jit(solution)/shard_map/all_gather | solution.py:113
  173.0 32.3 %all_gather.50 = bf16[1536,192]{1,0:T(8,128)(2,1)S(1)} all-gather(bf16[192,192]{1,0:T(8,128)(2,1)S(1)} %convert_element_type.179), channel_id=1, replica_groups=mesh['dp'=8,'mp'=4] {'dp'}, dimensions={0}, use_global_device_ids=true | all-gather | bytes 663552 | tf_op jit(solution)/shard_map/all_gather | solution.py:114
  205.3 32.0 %all_gather.48 = bf16[1536,192]{1,0:T(8,128)(2,1)S(1)} all-gather(bf16[192,192]{1,0:T(8,128)(2,1)S(1)} %convert_element_type.175), channel_id=1, replica_groups=mesh['dp'=8,'mp'=4] {'dp'}, dimensions={0}, use_global_device_ids=true | all-gather | bytes 663552 | tf_op jit(solution)/shard_map/all_gather | solution.py:115
  237.3 31.7 %all_gather.51 = bf16[192,1536]{0,1:T(8,128)(2,1)S(1)} all-gather(bf16[192,192]{0,1:T(8,128)(2,1)S(1)} %copy.28), channel_id=1, replica_groups=mesh['dp'=8,'mp'=4] {'dp'}, dimensions={1}, use_global_device_ids=true | all-gather | bytes 663552 | tf_op jit(solution)/shard_map/all_gather | solution.py:116
  270.7 3.2 fusion.79
  275.3 6.2 fusion.96
  286.3 3.3 fusion.91
  289.6 3.7 convolution_bitcast_fusion.1
  295.3 57.1 %reduce-scatter.14.cloned.1.call-done = f32[1,256,1536]{2,1,0:T(8,128)} async-done(((f32[1,1024,1536]{2,1,0:T(8,128)}), f32[1,256,1536]{2,1,0:T(8,128)}) %reduce-scatter.14.cloned.1.call-update) | async-done | bytes 1572880 | tf_op jit(solution)/shard_map/reduce_scatter | solution.py:46
  361.8 23.9 %all-gather.10.cloned.1.call-done = bf16[1,1024,1536]{2,1,0:T(8,128)(2,1)} async-done(((bf16[1,256,1536]{2,1,0:T(8,128)(2,1)}), bf16[1,1024,1536]{2,1,0:T(8,128)(2,1)}) %all-gather.10.cloned.1.call-update) | async-done | bytes 3145744 | tf_op jit(solution)/shard_map/all_gather | solution.py:42
  385.7 8.1 fusion.55
  393.8 54.5 %all-gather.12.cloned.1.call-done = bf16[1536,992]{1,0:T(8,128)(2,1)} async-done(((bf16[192,992]{1,0:T(8,128)(2,1)}), bf16[1536,992]{1,0:T(8,128)(2,1)}) %all-gather.12.cloned.1.call-update) | async-done | bytes 3047440 | tf_op jit(solution)/shard_map/all_gather | solution.py:119
  448.3 8.1 fusion.57
  456.4 21.1 %all-gather.18.cloned.1.call-done = bf16[1,1024,1536]{2,1,0:T(8,128)(2,1)} async-done(((bf16[1,256,1536]{2,1,0:T(8,128)(2,1)}), bf16[1,1024,1536]{2,1,0:T(8,128)(2,1)}) %all-gather.18.cloned.1.call-update) | async-done | bytes 3145744 | tf_op jit(solution)/shard_map/all_gather | solution.py:42
  477.5 62.2 %all-gather.16.cloned.1.call-done = bf16[992,1536]{0,1:T(8,128)(2,1)} async-done(((bf16[992,192]{0,1:T(8,128)(2,1)}), bf16[992,1536]{0,1:T(8,128)(2,1)}) %all-gather.16.cloned.1.call-update) | async-done | bytes 3047440 | tf_op jit(solution)/shard_map/all_gather | solution.py:121
  539.7 12.2 multiply_convert_fusion.1
  551.9 3.5 fusion.97
  555.4 5.8 add_bitcast_fusion.1
  561.3 9.8 convolution_bitcast_fusion
  571.3 47.6 %reduce-scatter.18.cloned.1.call-done = f32[1,256,1536]{2,1,0:T(8,128)} async-done(((f32[1,1024,1536]{2,1,0:T(8,128)}), f32[1,256,1536]{2,1,0:T(8,128)}) %reduce-scatter.18.cloned.1.call-update) | async-done | bytes 1572880 | tf_op jit(solution)/shard_map/reduce_scatter | solution.py:46
  621.8 58.4 %reduce-scatter.16.cloned.1.call-done = f32[1,256,1536]{2,1,0:T(8,128)} async-done(((f32[1,1024,1536]{2,1,0:T(8,128)}), f32[1,256,1536]{2,1,0:T(8,128)}) %reduce-scatter.16.cloned.1.call-update) | async-done | bytes 1572880 | tf_op jit(solution)/shard_map/reduce_scatter | solution.py:46
  680.2 4.8 fusion.94
  685.8 27.7 %all-gather.20.cloned.1.call-done = bf16[1,1024,1536]{2,1,0:T(8,128)(2,1)} async-done(((bf16[1,256,1536]{2,1,0:T(8,128)(2,1)}), bf16[1,1024,1536]{2,1,0:T(8,128)(2,1)}) %all-gather.20.cloned.1.call-update) | async-done | bytes 3145744 | tf_op jit(solution)/shard_map/all_gather | solution.py:42
  713.5 4.5 fusion.71
  718.1 3.1 fusion.85
  721.2 10.7 multiply_reduce_fusion
  734.0 6.4 multiply_convert_fusion
  748.5 3.8 add_bitcast_fusion
  752.7 8.7 fusion.53
  761.5 8.7 fusion.51
  770.3 8.6 fusion.47
  778.9 4.2 fusion.59
  783.4 4.1 fusion.61
  787.5 11.5 copy.33
  801.3 89.4 %while.7 = (s32[]{:T(128)}, f32[32,3]{0,1:T(4,128)S(1)}, s32[8,128,1024]{2,1,0:T(8,128)}, f32[8,3,128,1024]{3,1,2,0:T(4,128)}, s32[]{:T(128)}, /*index=5*/s32[]{:T(128)}) while((s32[]{:T(128)}, f32[32,3]{0,1:T(4,128)S(1)}, s32[8,128,1024]{2,1,0:T(8,128)}, f32[8,3,128,1024]{3,1,2,0:T(4,128)}, s32[]{:T(128)}, ...), condition=%wide.region_22.23_spmd.clone, body=%wide.region_21.22_spmd.clone.sunk | while | flops 155189440 | bytes 3671379 | solution.py:81
  802.4 10.1 fusion.143
  813.5 10.1 fusion.143
  824.7 10.1 fusion.143
  835.9 10.1 fusion.143
  847.1 10.1 fusion.143
  858.2 10.1 fusion.143
  869.4 10.1 fusion.143
  880.6 10.1 fusion.143
  890.7 22.7 %psum.7 = f32[32,3]{0,1:T(4,128)} all-reduce(f32[32,3]{0,1:T(4,128)S(1)} %get-tuple-element.127), channel_id=1, replica_groups=mesh['dp'=8,'mp'=4] {'dp'}, use_global_device_ids=true, to_apply=%region_23.24 | all-reduce | flops 96 | bytes 768 | tf_op jit(solution)/shard_map/psum | solution.py:239
  917.0 38.7 %all-reduce.4 = (f32[1536]{0:T(1024)S(1)}, f32[1536]{0:T(1024)S(1)}) all-reduce(f32[1536]{0:T(1024)S(1)} %get-tuple-element.157, f32[1536]{0:T(1024)S(1)} %copy-done.29), channel_id=6, replica_groups=mesh['dp'=8,'mp'=4] {'dp','mp'}, use_global_device_ids=true, to_apply=%region_14.15.clone | all-reduce | flops 3072 | bytes 24576
  956.9 3.0 fusion.75
  959.8 7.4 reduce-scatter.28.cloned.1.call-done
  967.2 121.3 %reduce-scatter.30.cloned.1.call-done = f32[192,992]{1,0:T(8,128)} async-done(((f32[1536,992]{1,0:T(8,128)}), f32[192,992]{1,0:T(8,128)}) %reduce-scatter.30.cloned.1.call-update) | async-done | bytes 761872 | tf_op jit(solution)/shard_map/reduce_scatter | solution.py:250
  1088.5 121.3 %reduce-scatter.32.cloned.1.call-done = f32[992,192]{0,1:T(8,128)} async-done(((f32[992,1536]{0,1:T(8,128)}), f32[992,192]{0,1:T(8,128)}) %reduce-scatter.32.cloned.1.call-update) | async-done | bytes 761872 | tf_op jit(solution)/shard_map/reduce_scatter | solution.py:251
  1209.8 69.1 %reduce-scatter.26.cloned.1.call-done = f32[192,192]{1,0:T(8,128)} async-done(((f32[1536,192]{1,0:T(8,128)}), f32[192,192]{1,0:T(8,128)}) %reduce-scatter.26.cloned.1.call-update) | async-done | bytes 147472 | tf_op jit(solution)/shard_map/reduce_scatter | solution.py:247
  1278.9 68.4 %reduce-scatter.24.cloned.1.call-done = f32[192,192]{1,0:T(8,128)} async-done(((f32[1536,192]{1,0:T(8,128)}), f32[192,192]{1,0:T(8,128)}) %reduce-scatter.24.cloned.1.call-update) | async-done | bytes 147472 | tf_op jit(solution)/shard_map/reduce_scatter | solution.py:246
  1347.3 68.5 %reduce-scatter.22.cloned.1.call-done = f32[192,192]{1,0:T(8,128)} async-done(((f32[1536,192]{1,0:T(8,128)}), f32[192,192]{1,0:T(8,128)}) %reduce-scatter.22.cloned.1.call-update) | async-done | bytes 147472 | tf_op jit(solution)/shard_map/reduce_scatter | solution.py:245
  (186 shorter events, 65.7 us)
Async XLA Ops:
  8.0 262.6 %all-gather.8.cloned.1.call-start = ((), (), s32[]{:S(2)}) async-start(), calls=%async_computation.11 | async-start | bytes 3932160 | tf_op jit(solution)/shard_map/all_gather | solution.py:42
  51.9 2.1 copy-start.26
  53.5 0.5 copy-start.33
  54.0 0.6 copy-start.31
  54.6 8.7 copy-start.21
  57.1 6.2 copy-start.22
  57.1 6.2 copy-start.37
  57.2 295.3 %reduce-scatter.14.cloned.1.call-start = ((), (), s32[]{:S(2)}) async-start(), calls=%async_computation.12 | async-start | bytes 7864320 | tf_op jit(solution)/shard_map/reduce_scatter | solution.py:46
  122.9 17.7 %copy-start.23 = (f32[192,192]{1,0:T(8,128)S(1)}, f32[192,192]{1,0:T(8,128)}, u32[]{:S(2)}) copy-start(f32[192,192]{1,0:T(8,128)} %param.23) | copy-start | bytes 442372
  122.9 17.7 %copy-start.24 = (f32[192,192]{1,0:T(8,128)S(1)}, f32[192,192]{1,0:T(8,128)}, u32[]{:S(2)}) copy-start(f32[192,192]{1,0:T(8,128)} %param.24) | copy-start | bytes 442372
  140.6 128.5 %copy-start.30 = (s32[1,1024]{1,0:T(1,128)S(1)}, s32[1,1024]{1,0:T(1,128)}, u32[]{:S(2)}) copy-start(s32[1,1024]{1,0:T(1,128)} %param.18) | copy-start | bytes 12292
  173.0 100.9 %copy-start.9 = (bf16[1536,192]{1,0:T(8,128)(2,1)}, bf16[1536,192]{1,0:T(8,128)(2,1)S(1)}, u32[]{:S(2)}) copy-start(bf16[1536,192]{1,0:T(8,128)(2,1)S(1)} %all_gather.49) | copy-start | bytes 1769476
  205.3 68.6 %copy-start.11 = (bf16[1536,192]{1,0:T(8,128)(2,1)}, bf16[1536,192]{1,0:T(8,128)(2,1)S(1)}, u32[]{:S(2)}) copy-start(bf16[1536,192]{1,0:T(8,128)(2,1)S(1)} %all_gather.50) | copy-start | bytes 1769476
  237.3 47.1 %copy-start.5 = (bf16[1536,192]{1,0:T(8,128)(2,1)}, bf16[1536,192]{1,0:T(8,128)(2,1)S(1)}, u32[]{:S(2)}) copy-start(bf16[1536,192]{1,0:T(8,128)(2,1)S(1)} %all_gather.48) | copy-start | bytes 1769476
  269.0 20.6 %copy-start.7 = (bf16[192,1536]{0,1:T(8,128)(2,1)}, bf16[192,1536]{0,1:T(8,128)(2,1)S(1)}, u32[]{:S(2)}) copy-start(bf16[192,1536]{0,1:T(8,128)(2,1)S(1)} %all_gather.51) | copy-start | bytes 1769476
  270.7 3.2 copy-start.3
  273.9 7.6 copy-start.15
  273.9 1.4 copy-start.14
  281.5 4.5 copy-start
  281.5 4.7 copy-start.25
  284.4 5.2 copy-start.28
  285.6 4.0 copy-start.18
  289.6 3.7 copy-start.17
  293.3 1.1 copy-start.20
  293.3 59.1 %copy-start.2 = (f32[1,256,1536]{2,1,0:T(8,128)S(1)}, f32[1,256,1536]{2,1,0:T(8,128)}, u32[]{:S(2)}) copy-start(f32[1,256,1536]{2,1,0:T(8,128)} %param.17) | copy-start | bytes 4718596
  293.3 68.4 %all-gather.14.cloned.1.call-start = ((), (), s32[]{:S(2)}) async-start(), calls=%async_computation.15 | async-start | bytes 3538944 | tf_op jit(solution)/shard_map/all_gather | solution.py:120
  295.3 90.4 %all-gather.10.cloned.1.call-start = ((), (), s32[]{:S(2)}) async-start(), calls=%async_computation.13 | async-start | bytes 3932160 | tf_op jit(solution)/shard_map/all_gather | solution.py:42
  355.2 93.1 %all-gather.12.cloned.1.call-start = ((), (), s32[]{:S(2)}) async-start(), calls=%async_computation.14 | async-start | bytes 3538944 | tf_op jit(solution)/shard_map/all_gather | solution.py:119
  357.2 120.3 %all-gather.18.cloned.1.call-start = ((), (), s32[]{:S(2)}) async-start(), calls=%async_computation.18 | async-start | bytes 3932160 | tf_op jit(solution)/shard_map/all_gather | solution.py:42
  359.7 180.0 %all-gather.16.cloned.1.call-start = ((), (), s32[]{:S(2)}) async-start(), calls=%async_computation.16 | async-start | bytes 3538944 | tf_op jit(solution)/shard_map/all_gather | solution.py:121
  361.7 257.2 %reduce-scatter.18.cloned.1.call-start = ((), (), s32[]{:S(2)}) async-start(), calls=%async_computation.19 | async-start | bytes 7864320 | tf_op jit(solution)/shard_map/reduce_scatter | solution.py:46
  539.6 12.2 copy-start.36
  551.9 3.5 copy-start.39
  551.9 3.5 copy-start.38
  551.9 3.5 copy-start.35
  561.2 118.9 %reduce-scatter.16.cloned.1.call-start = ((), (), s32[]{:S(2)}) async-start(), calls=%async_computation.17 | async-start | bytes 7864320 | tf_op jit(solution)/shard_map/reduce_scatter | solution.py:46
  571.0 142.4 %all-gather.20.cloned.1.call-start = ((), (), s32[]{:S(2)}) async-start(), calls=%async_computation.20 | async-start | bytes 3932160 | tf_op jit(solution)/shard_map/all_gather | solution.py:42
  684.9 228.5 %reduce-scatter.34.cloned.1.call-start = ((), (), s32[]{:S(2)}) async-start(), calls=%async_computation.28 | async-start | bytes 1769472
  685.8 32.3 %copy-start.8 = (bf16[192,1536]{0,1:T(8,128)(2,1)S(1)}, bf16[192,1536]{0,1:T(8,128)(2,1)}, u32[]{:S(2)}) copy-start(bf16[192,1536]{0,1:T(8,128)(2,1)} %copy-done.7) | copy-start | bytes 1769476
  718.0 3.2 copy-start.19
  718.0 197.2 %reduce-scatter.20.cloned.1.call-start = ((), (), s32[]{:S(2)}) async-start(), calls=%async_computation.21 | async-start | bytes 7864320 | tf_op jit(solution)/shard_map/reduce_scatter | solution.py:46
  721.2 10.7 slice-start
  721.2 11.2 slice-start.1
  721.2 12.8 slice-start.2
  734.0 6.4 copy-start.16
  740.4 2.8 copy-start.1
  740.4 1.7 copy-start.12
  743.2 2.0 copy-start.10
  746.3 2.2 copy-start.6
  752.3 215.0 %reduce-scatter.28.cloned.1.call-start = ((), (), s32[]{:S(2)}) async-start(), calls=%async_computation.25 | async-start | bytes 7077888 | tf_op jit(solution)/shard_map/reduce_scatter | solution.py:249
  761.4 327.1 %reduce-scatter.30.cloned.1.call-start = ((), (), s32[]{:S(2)}) async-start(), calls=%async_computation.26 | async-start | bytes 7077888 | tf_op jit(solution)/shard_map/reduce_scatter | solution.py:250
  770.2 439.6 %reduce-scatter.32.cloned.1.call-start = ((), (), s32[]{:S(2)}) async-start(), calls=%async_computation.27 | async-start | bytes 7077888 | tf_op jit(solution)/shard_map/reduce_scatter | solution.py:251
  778.9 500.0 %reduce-scatter.26.cloned.1.call-start = ((), (), s32[]{:S(2)}) async-start(), calls=%async_computation.24 | async-start | bytes 1769472 | tf_op jit(solution)/shard_map/reduce_scatter | solution.py:247
  783.1 564.1 %reduce-scatter.24.cloned.1.call-start = ((), (), s32[]{:S(2)}) async-start(), calls=%async_computation.23 | async-start | bytes 1769472 | tf_op jit(solution)/shard_map/reduce_scatter | solution.py:246
  787.5 628.3 %reduce-scatter.22.cloned.1.call-start = ((), (), s32[]{:S(2)}) async-start(), calls=%async_computation.22 | async-start | bytes 1769472 | tf_op jit(solution)/shard_map/reduce_scatter | solution.py:245
  787.5 11.5 copy-start.4
  801.2 114.0 %copy-start.27 = (f32[1536]{0:T(1024)S(1)}, f32[1536]{0:T(1024)}, u32[]{:S(2)}) copy-start(f32[1536]{0:T(1024)} %copy-done.26) | copy-start | bytes 18436
  801.2 114.0 %copy-start.32 = (f32[256]{0:T(256)S(1)}, f32[256]{0:T(256)}, u32[]{:S(2)}) copy-start(f32[256]{0:T(256)} %copy-done.31) | copy-start | bytes 3076
  890.7 26.3 %copy-start.29 = (f32[1536]{0:T(1024)S(1)}, f32[1536]{0:T(1024)}, u32[]{:S(2)}) copy-start(f32[1536]{0:T(1024)} %get-tuple-element.155) | copy-start | bytes 18436
  890.7 66.1 %copy-start.34 = (f32[256]{0:T(256)S(1)}, f32[256]{0:T(256)}, u32[]{:S(2)}) copy-start(f32[256]{0:T(256)} %copy-done.33) | copy-start | bytes 3076
  890.7 66.1 %copy-start.13 = (f32[1,256,1536]{2,1,0:T(8,128)S(1)}, f32[1,256,1536]{2,1,0:T(8,128)}, u32[]{:S(2)}) copy-start(f32[1,256,1536]{2,1,0:T(8,128)} %get-tuple-element.180) | copy-start | bytes 4718596
Sparse Core Ops, SparseCore 0:
  57.3 28.3 all-gather.7
  293.5 58.9 reduce-scatter.13
  561.3 57.4 reduce-scatter.17
  621.3 58.8 reduce-scatter.15
Sparse Core Ops, SparseCore 1:
  296.6 60.0 all-gather.13
  358.6 27.0 all-gather.9
  388.3 59.9 all-gather.11
  450.4 27.0 all-gather.17
  479.7 59.9 all-gather.15
  685.0 28.4 all-gather.19
  718.1 65.5 reduce-scatter.33
  786.0 57.6 reduce-scatter.19
  847.7 119.5 reduce-scatter.27
  971.4 117.0 reduce-scatter.29
  1092.5 117.2 reduce-scatter.31
  1213.8 65.0 reduce-scatter.25
  1282.7 64.5 reduce-scatter.23
  1351.3 64.5 reduce-scatter.21
where the time goes:
time: 1430 us; the launch traced here: 1420 us
  waiting for transfers between devices  809 us (57%)
  matrix products  263 us (18%)
  blocking collectives  232 us (16%)
  local copies, waits for them, and re-layouts  55.5 us (4%)
  other arithmetic  45.5 us (3%)
  between operations  16.4 us (1%)
    reduce_scatter x4, waiting for transfers between devices, spread(): return lax.psum_scatter(part, 'mp', scatter_dimension=1, tiled=True)  163 us
    reduce_scatter x1, waiting for transfers between devices, local(): lax.psum_scatter(down_term, 'dp', scatter_dimension=1, tiled=True)  121 us
    reduce_scatter x1, waiting for transfers between devices, local(): lax.psum_scatter(lift_term, 'dp', scatter_dimension=0, tiled=True)  121 us
    unnamed x2, blocking collectives  80.7 us
    dot_general x8, matrix products, table_one_block(): jnp.einsum('bij,hij->bh', onehot, piece, precision=HIGHEST)  80.6 us
    all_gather x4, waiting for transfers between devices, collect(): return lax.all_gather(part, 'mp', axis=1, tiled=True)  72.7 us
    reduce_scatter x1, waiting for transfers between devices, local(): lax.psum_scatter(value_term, 'dp', scatter_dimension=0, tiled=True)  69.1 us
    reduce_scatter x1, waiting for transfers between devices, local(): lax.psum_scatter(query_term, 'dp', scatter_dimension=0, tiled=True)  68.5 us
  transfers between devices with their start and end apart: 18, of which 14 were waited for; matrix products, arithmetic and copies ran while one was open for 21% of the time, Pallas kernels for 0%

commit v1 on v0

--- a/solution.py
+++ b/solution.py
@@ -1,9 +1,1069 @@
+import functools
+
 import jax
 import jax.numpy as jnp
 from jax import lax
+from jax.experimental import pallas as pl
+from jax.experimental.pallas import tpu as pltpu
 from jax.sharding import PartitionSpec as P
 
 EPSILON = 1e-06
+MESH = pl.DeviceIdType.MESH
+BF16 = jnp.bfloat16
+F32 = jnp.float32
+VMEM_SPEC = pl.BlockSpec(memory_space=pltpu.VMEM)
+ANY_SPEC = pl.BlockSpec(memory_space=pl.ANY)
+DMA = pltpu.SemaphoreType.DMA
+
+
+def remote(source, target, send_sem, recv_sem, where):
+    return pltpu.make_async_remote_copy(
+        src_ref=source,
+        dst_ref=target,
+        send_sem=send_sem,
+        recv_sem=recv_sem,
+        device_id=where,
+        device_id_type=MESH,
+    )
+
+
+def matmul(left, right):
+    return lax.dot_general(left, right, (((1,), (0,)), ((), ())), preferred_element_type=F32)
+
+
+def matmul_nt(left, right):
+    return lax.dot_general(left, right, (((1,), (1,)), ((), ())), preferred_element_type=F32)
+
+
+def matmul_tn(left, right):
+    return lax.dot_general(left, right, (((0,), (0,)), ((), ())), preferred_element_type=F32)
+
+
+class Place:
+    def __init__(self, n):
+        self.n = n
+        self.d = lax.axis_index("dp")
+        self.m = lax.axis_index("mp")
+        self.pos = lax.rem(self.d, 2) * (n - 1) + (self.d // 2) * (1 - 2 * lax.rem(self.d, 2))
+        self.right = self.device(self.pos + 1)
+        self.left = self.device(self.pos + n - 1)
+        self.mate = self.m + 1 - 2 * lax.rem(self.m, 2)
+        self.twin = lax.rem(self.m + 2, 4)
+        self.far = lax.rem(self.mate + 2, 4)
+
+    def device(self, position):
+        position = lax.rem(position, self.n)
+        late = position // (self.n // 2)
+        return 2 * position * (1 - late) + (2 * (self.n - 1 - position) + 1) * late
+
+    def barrier(self, ring=True, pair=True, everyone=False):
+        sem = pltpu.get_barrier_semaphore()
+        partners = []
+        if everyone:
+            partners += [{"dp": lax.rem(self.d + k, self.n)} for k in range(1, self.n)]
+        elif ring:
+            partners += [{"dp": self.right}, {"dp": self.left}]
+        if pair:
+            partners += [{"mp": self.mate}, {"mp": self.twin}, {"mp": self.far}]
+        for where in partners:
+            pl.semaphore_signal(sem, inc=1, device_id=where, device_id_type=MESH)
+        pl.semaphore_wait(sem, len(partners))
+
+
+class RingGather:
+    def __init__(self, place, full, send, recv):
+        self.place, self.full, self.send, self.recv = place, full, send, recv
+        self.steps = place.n // 2
+
+    def part(self, way, position, step):
+        slot = self.full.at[self.place.device(position + self.place.n)]
+        if step < self.steps - 1:
+            return slot
+        half = self.full.shape[1] // 2
+        return slot.at[pl.ds(half * way, half)]
+
+    def outgoing(self, way, step):
+        ref = self.part(way, self.place.pos + (step if way else -step), step)
+        where = {"dp": self.place.left if way else self.place.right}
+        return remote(ref, ref, self.send.at[way, step], self.recv.at[way, step], where)
+
+    def incoming(self, way, step):
+        ref = self.part(way, self.place.pos + (1 + step if way else -1 - step), step)
+        where = {"dp": self.place.left if way else self.place.right}
+        return remote(ref, ref, self.send.at[way, step], self.recv.at[way, step], where)
+
+    def advance(self, way, step):
+        if step:
+            self.incoming(way, step - 1).wait_recv()
+        if step < self.steps:
+            self.outgoing(way, step).start()
+
+    def finish(self):
+        for way in (0, 1):
+            for step in range(self.steps):
+                self.outgoing(way, step).wait_send()
+
+
+class PairGather:
+    def __init__(self, place, full, send, recv, chunks=2):
+        self.place, self.full, self.send, self.recv, self.chunks = place, full, send, recv, chunks
+
+    def rows(self, owner, chunk):
+        size = self.full.shape[0] // 4
+        part = size // self.chunks
+        return self.full.at[pl.ds(pl.multiple_of(owner * size + chunk * part, part), part)]
+
+    def copy(self, kind, chunk, owner):
+        where = {"mp": self.place.twin if kind == 1 else self.place.mate}
+        ref = self.rows(owner, chunk)
+        return remote(ref, ref, self.send.at[kind, chunk], self.recv.at[kind, chunk], where)
+
+    def begin(self, chunk):
+        self.copy(1, chunk, self.place.m).start()
+        self.copy(0, chunk, self.place.m).start()
+
+    def relay(self, chunk):
+        self.copy(1, chunk, self.place.twin).wait_recv()
+        self.copy(2, chunk, self.place.twin).start()
+
+    def end(self, chunk):
+        self.copy(0, chunk, self.place.mate).wait_recv()
+        self.copy(2, chunk, self.place.far).wait_recv()
+        for kind in range(3):
+            self.copy(kind, chunk, self.place.m).wait_send()
+
+
+def norm_scale(values):
+    return lax.rsqrt(jnp.mean(values * values, axis=-1, keepdims=True) + EPSILON)
+
+
+class PairScatter:
+    def __init__(self, place, give, got, over, came, send, recv, chunks=2):
+        self.place, self.chunks = place, chunks
+        self.give, self.got, self.over, self.came = give, got, over, came
+        self.send, self.recv = send, recv
+
+    def rows(self, chunk):
+        part = self.over.shape[0] // self.chunks
+        return pl.ds(chunk * part, part)
+
+    def copy(self, kind, chunk):
+        rows = self.rows(chunk)
+        if kind == 2:
+            source, target, where = self.over.at[rows], self.came.at[rows], {"mp": self.place.twin}
+        else:
+            source, target, where = self.give.at[kind, rows], self.got.at[kind, rows], {"mp": self.place.mate}
+        return remote(source, target, self.send.at[kind, chunk], self.recv.at[kind, chunk], where)
+
+    def far(self, value):
+        self.give[0] = value.astype(BF16)
+        for chunk in range(self.chunks):
+            self.copy(0, chunk).start()
+
+    def twin(self, value):
+        part = self.over.shape[0] // self.chunks
+        for chunk in range(self.chunks):
+            rows = self.rows(chunk)
+            self.copy(0, chunk).wait_recv()
+            mine = value[chunk * part : (chunk + 1) * part]
+            self.over[rows, :] = (mine + self.got[0, rows, :].astype(F32)).astype(BF16)
+            self.copy(2, chunk).start()
+
+    def mate(self, value):
+        self.give[1] = value.astype(BF16)
+        for chunk in range(self.chunks):
+            self.copy(1, chunk).start()
+
+    def take(self, chunk, value):
+        rows = self.rows(chunk)
+        self.copy(1, chunk).wait_recv()
+        self.copy(2, chunk).wait_recv()
+        return value + self.got[1, rows, :].astype(F32) + self.came[rows, :].astype(F32)
+
+    def finish(self):
+        for kind in range(3):
+            for chunk in range(self.chunks):
+                self.copy(kind, chunk).wait_send()
+
+    @staticmethod
+    def scratch(rows, columns, chunks=2):
+        return [
+            pltpu.VMEM((2, rows, columns), BF16), pltpu.VMEM((2, rows, columns), BF16),
+            pltpu.VMEM((rows, columns), BF16), pltpu.VMEM((rows, columns), BF16),
+            DMA((3, chunks)), DMA((3, chunks)),
+        ]
+
+
+class RingScatter:
+    def __init__(self, place, term, out, put, inbox, send, recv):
+        self.place, self.term, self.out, self.put, self.inbox = place, term, out, put, inbox
+        self.send, self.recv = send, recv
+        self.steps = place.n // 2
+
+    def copy(self, way, step):
+        source, target = self.put.at[way, step], self.inbox.at[way, step]
+        if step == 0:
+            half = source.shape[0] // 2
+            rows = pl.ds(half * way, half)
+            source, target = source.at[rows], target.at[rows]
+        where = {"dp": self.place.left if way else self.place.right}
+        return remote(source, target, self.send.at[way, step], self.recv.at[way, step], where)
+
+    def arrived(self, way, step, total):
+        self.copy(way, step).wait_recv()
+        if step:
+            return total + self.inbox[way, step].astype(F32)
+        half = total.shape[0] // 2
+        if way:
+            return jnp.concatenate([total[:half], total[half:] + self.inbox[way, 0, half:, :].astype(F32)], axis=0)
+        return jnp.concatenate([total[:half] + self.inbox[way, 0, :half, :].astype(F32), total[half:]], axis=0)
+
+    def advance(self, way, step):
+        n = self.place.n
+        away = self.steps - step
+        owner = self.place.device(self.place.pos + (n - away if way else away))
+        total = self.term(owner)
+        if step:
+            total = self.arrived(way, step - 1, total)
+        self.put[way, step] = total.astype(BF16)
+        self.copy(way, step).start()
+
+    def finish(self):
+        total = self.term(self.place.d)
+        for way in (0, 1):
+            total = self.arrived(way, self.steps - 1, total)
+        self.out[...] = total
+        for way in (0, 1):
+            for step in range(self.steps):
+                self.copy(way, step).wait_send()
+
+    @staticmethod
+    def scratch(n, rows, columns):
+        return [
+            pltpu.VMEM((2, n // 2, rows, columns), BF16), pltpu.VMEM((2, n // 2, rows, columns), BF16),
+            DMA((2, n // 2)), DMA((2, n // 2)),
+        ]
+
+
+def slot_columns(ref, slot, n):
+    width = ref.shape[1] // n
+    pair = ref[:, pl.ds(pl.multiple_of((slot // 2) * (2 * width), 2 * width), 2 * width)]
+    return jnp.where(lax.rem(slot, 2) == 0, pair[:, :width], pair[:, width:])
+
+
+def gate_terms(gate):
+    square = gate * gate
+    inner = 0.7978845608 * (gate + 0.044715 * (square * gate))
+    bend = jnp.tanh(inner)
+    half = 0.5 * (1.0 + bend)
+    slope = half + 0.5 * gate * (1.0 - bend * bend) * (0.7978845608 * (1.0 + 0.134145 * square))
+    return gate * half, slope
+
+
+def bias_tiles(row_ref, tiles_ref):
+    heads, kinds, block, _ = tiles_ref.shape
+    for h in range(heads):
+        for t in range(kinds):
+            line = jnp.broadcast_to(row_ref[pl.ds(h * kinds + t, 1), :], (block, 2 * block))
+            if t in (0, kinds - 1):
+                tiles_ref[h, t] = line[:, :block]
+            else:
+                tiles_ref[h, t] = pltpu.roll(line, 0, 1, stride=1, stride_axis=0)[:, :block]
+
+
+def key_window(seg_smem, index, block, count):
+    first, last = seg_smem[0, index * block], seg_smem[0, index * block + block - 1]
+    low, high = jnp.int32(0), jnp.int32(0)
+    for j in range(count):
+        low += (seg_smem[0, j * block + block - 1] < first).astype(jnp.int32)
+        high += (seg_smem[0, j * block] <= last).astype(jnp.int32)
+    return low, high - low
+
+
+def score_block(query, key_rows, tile, same):
+    return jnp.where(same, matmul_nt(query, key_rows) + tile, -1e30)
+
+
+def attend_kernel(seg_smem, qkv_ref, segr_ref, segc_ref, tiles_ref, ctx_ref, ctx32_ref, lse_ref):
+    heads, _, block, _ = tiles_ref.shape
+    length, width = qkv_ref.shape
+    width = width // (3 * heads)
+    count = length // block
+
+    def run(index, low, blocks):
+        rows = pl.ds(pl.multiple_of(index * block, block), block)
+        seg_q = segc_ref[rows, :]
+        places, sames, tile_at = [], [], []
+        for t in range(blocks):
+            j = low + t
+            place = pl.ds(pl.multiple_of(j * block, block), block)
+            places.append(place)
+            sames.append(seg_q == segr_ref[:, place])
+            tile_at.append(jnp.clip(j - index, -2, 2) + 2)
+        outs, logs = [], []
+        for h in range(heads):
+            lanes = slice(h * width, (h + 1) * width)
+            query = qkv_ref[rows, :][:, lanes]
+            scores = []
+            for t in range(blocks):
+                key_rows = qkv_ref[places[t], :][:, heads * width + h * width : heads * width + (h + 1) * width]
+                scores.append(score_block(query, key_rows, tiles_ref[h, tile_at[t]], sames[t]))
+            peak = functools.reduce(jnp.maximum, scores)
+            peak = jnp.max(peak, axis=1, keepdims=True)
+            raised = [jnp.exp(s - peak) for s in scores]
+            total = jnp.sum(functools.reduce(jnp.add, raised), axis=1, keepdims=True)
+            scale = 1.0 / total
+            context = jnp.zeros((block, width), F32)
+            for t in range(blocks):
+                value_rows = qkv_ref[places[t], :][:, 2 * heads * width + h * width : 2 * heads * width + (h + 1) * width]
+                context += matmul((raised[t] * scale).astype(BF16), value_rows)
+            outs.append(context)
+            logs.append(peak + jnp.log(total))
+        context = jnp.concatenate(outs, axis=1)
+        ctx32_ref[rows, :] = context
+        ctx_ref[rows, :] = context.astype(BF16)
+        lse_ref[rows, :] = jnp.concatenate(logs + [jnp.zeros((block, 8 - heads), F32)], axis=1)
+
+    @pl.loop(0, count)
+    def _(index):
+        low, many = key_window(seg_smem, index, block, count)
+        for blocks in range(1, count + 1):
+            pl.when(many == blocks)(functools.partial(run, index, low, blocks))
+
+
+def attend(qkv, segments, tiles):
+    length, width = qkv.shape
+    heads = tiles.shape[0]
+    return pl.pallas_call(
+        attend_kernel,
+        name="attend",
+        out_shape=(
+            jax.ShapeDtypeStruct((length, width // 3), BF16),
+            jax.ShapeDtypeStruct((length, width // 3), F32),
+            jax.ShapeDtypeStruct((length, 8), F32),
+        ),
+        in_specs=[pl.BlockSpec(memory_space=pltpu.SMEM)] + [VMEM_SPEC] * 4,
+        out_specs=(VMEM_SPEC,) * 3,
+    )(segments, qkv, segments, segments.reshape(length, 1), tiles)
+
+
+def attend_back_kernel(
+    seg_smem, qkv_ref, segr_ref, segc_ref, tiles_ref, ctx32_ref, lse_ref, mixed_ref, wmix_ref, buckets_ref,
+    cots_ref, table_ref, do_ref, dk_ref, dv_ref, sums_ref,
+):
+    heads, kinds, block, _ = tiles_ref.shape
+    length, width = qkv_ref.shape
+    width = width // (3 * heads)
+    count = length // block
+    dk_ref[...] = jnp.zeros_like(dk_ref)
+    dv_ref[...] = jnp.zeros_like(dv_ref)
+    sums_ref[...] = jnp.zeros_like(sums_ref)
+
+    @pl.loop(0, count)
+    def _(index):
+        rows = pl.ds(pl.multiple_of(index * block, block), block)
+        weight = wmix_ref[...].reshape(-1, heads * width)
+        do_ref[rows, :] = matmul(mixed_ref[rows, :], weight).astype(BF16)
+
+    def run(index, low, blocks):
+        rows = pl.ds(pl.multiple_of(index * block, block), block)
+        seg_q = segc_ref[rows, :]
+        places, sames, tile_at = [], [], []
+        for t in range(blocks):
+            j = low + t
+            place = pl.ds(pl.multiple_of(j * block, block), block)
+            places.append(place)
+            sames.append(seg_q == segr_ref[:, place])
+            tile_at.append(jnp.clip(j - index, -2, 2) + 2)
+        product = do_ref[rows, :].astype(F32) * ctx32_ref[rows, :]
+        logs = lse_ref[rows, :]
+        outs = []
+        for h in range(heads):
+            lanes = slice(h * width, (h + 1) * width)
+            query = qkv_ref[rows, :][:, lanes]
+            grad = do_ref[rows, :][:, lanes]
+            inner = jnp.sum(product[:, lanes], axis=1, keepdims=True)
+            log = logs[:, h : h + 1]
+            query_cot = jnp.zeros((block, width), F32)
+            for t in range(blocks):
+                here = qkv_ref[places[t], :]
+                key_rows = here[:, heads * width + h * width : heads * width + (h + 1) * width]
+                value_rows = here[:, 2 * heads * width + h * width : 2 * heads * width + (h + 1) * width]
+                probs = jnp.exp(score_block(query, key_rows, tiles_ref[h, tile_at[t]], sames[t]) - log)
+                prob_cot = matmul_nt(grad, value_rows)
+                cot = (probs * (prob_cot - inner)).astype(BF16)
+                dv_ref[h, places[t], :] += matmul_tn(probs.astype(BF16), grad)
+                dk_ref[h, places[t], :] += matmul_tn(cot, query)
+                query_cot += matmul(cot, key_rows)
+                sums_ref[h, tile_at[t]] += cot.astype(F32)
+            outs.append(query_cot)
+        cots_ref[rows, : heads * width] = jnp.concatenate(outs, axis=1).astype(BF16)
+
+    @pl.loop(0, count)
+    def _(index):
+        low, many = key_window(seg_smem, index, block, count)
+        for blocks in range(1, count + 1):
+            pl.when(many == blocks)(functools.partial(run, index, low, blocks))
+
+    both = [dk_ref[h] for h in range(heads)] + [dv_ref[h] for h in range(heads)]
+    cots_ref[:, heads * width :] = jnp.concatenate(both, axis=1).astype(BF16)
+    lines = []
+    for h in range(heads):
+        for t in range(kinds):
+            if t in (0, kinds - 1):
+                line = jnp.sum(sums_ref[h, t], axis=0, keepdims=True)
+                lines.append(jnp.concatenate([line, jnp.zeros_like(line)], axis=1))
+                continue
+
+            def shifted(group, total):
+                eight = sums_ref[h, t, pl.ds(pl.multiple_of(group * 8, 8), 8), :]
+                wide = jnp.concatenate([eight, jnp.zeros_like(eight)], axis=1)
+                return total + pltpu.roll(wide, lax.rem(2 * block - 8 * group, 2 * block), 1)
+
+            total = lax.fori_loop(0, block // 8, shifted, jnp.zeros((8, 2 * block), F32))
+            place = lax.broadcasted_iota(jnp.int32, total.shape, 0)
+            for bit in (1, 2, 4):
+                total = jnp.where((place // bit) % 2 == 1, pltpu.roll(total, 2 * block - bit, 1), total)
+            lines.append(jnp.sum(total, axis=0, keepdims=True))
+    total = jnp.zeros(table_ref.shape, F32)
+    for t in range(kinds):
+        line = jnp.concatenate([lines[h * kinds + t] for h in range(heads)] + [jnp.zeros((8 - heads, 2 * block), F32)], axis=0)
+        total += lax.dot_general(
+            line, buckets_ref[t], (((1,), (0,)), ((), ())), precision=lax.Precision.HIGHEST, preferred_element_type=F32
+        )
+    table_ref[...] = total
+
+
+def attend_back(qkv, segments, tiles, ctx32, lse, mixed, wmix, buckets):
+    length, width = qkv.shape
+    heads, _, block, _ = tiles.shape
+    size = width // (3 * heads)
+    return pl.pallas_call(
+        attend_back_kernel,
+        name="attend_back",
+        out_shape=(
+            jax.ShapeDtypeStruct((length, width), BF16),
+            jax.ShapeDtypeStruct((8, 128), F32),
+        ),
+        in_specs=[pl.BlockSpec(memory_space=pltpu.SMEM)] + [VMEM_SPEC] * 9,
+        out_specs=(VMEM_SPEC,) * 2,
+        scratch_shapes=[
+            pltpu.VMEM((length, width // 3), BF16),
+            pltpu.VMEM((heads, length, size), F32),
+            pltpu.VMEM((heads, length, size), F32),
+            pltpu.VMEM((heads, 5, block, block), F32),
+        ],
+    )(segments, qkv, segments, segments.reshape(length, 1), tiles, ctx32, lse, mixed, wmix, buckets)
+
+
+def block_rows(place, owner, size):
+    return pl.ds(pl.multiple_of(owner * size, size), size)
+
+
+def gain_lanes(n, shape):
+    row = lax.broadcasted_iota(jnp.int32, shape, 0)
+    lane = lax.broadcasted_iota(jnp.int32, shape, 1)
+    count = shape[1] // (4 * n)
+    shift = (row // 8) * count
+    inside = (lane >= shift) & (lane < shift + count)
+    return inside, row - 8 * (row // 8)
+
+
+def enter_kernel(
+    n, x_ref, cot_ref, gain_ref, spread_ref, w_ref, wgate_ref, line_ref,
+    normed_out, cot_out, wgate_out, qkv_ref, wqkv_ref, wmix_ref, gains_ref, tiles_ref,
+    wfull, gfull, nfull, cfull, g4, g32,
+    ring_send, ring_recv, gate_send, gate_recv, pair_send, pair_recv, cot_send, cot_recv,
+    g_send, g_recv, h_send, h_recv, local_sem,
+):
+    place = Place(n)
+    size = x_ref.shape[0]
+    own_w = pltpu.make_async_copy(w_ref, wfull.at[place.d], local_sem.at[0])
+    own_g = pltpu.make_async_copy(gain_ref, g4.at[place.m], local_sem.at[1])
+    own_gate = pltpu.make_async_copy(wgate_ref, gfull.at[place.d], local_sem.at[2])
+    for copy in (own_w, own_g, own_gate):
+        copy.start()
+    place.barrier(everyone=True)
+    ring = RingGather(place, wfull, ring_send, ring_recv)
+    gate_ring = RingGather(place, gfull, gate_send, gate_recv)
+    small = [
+        remote(gain_ref, g4.at[place.m], g_send.at[k], g_recv.at[k], {"mp": lax.rem(place.m + k, 4)})
+        for k in range(1, 4)
+    ]
+    for copy in small:
+        copy.start()
+    own_w.wait()
+    own_gate.wait()
+    for way in (0, 1):
+        ring.advance(way, 0)
+    scale = norm_scale(x_ref[...])
+    rows = block_rows(place, place.m, size)
+    cfull[rows, :] = cot_ref[...].astype(BF16)
+    own_g.wait()
+    for k in range(1, 4):
+        slot = g4.at[lax.rem(place.m + 4 - k, 4)]
+        remote(slot, slot, g_send.at[k], g_recv.at[k], {"mp": place.mate}).wait_recv()
+    around = [
+        remote(g4, g32.at[place.d], h_send.at[k], h_recv.at[k], {"dp": lax.rem(place.d + k, n)})
+        for k in range(1, n)
+    ]
+    for copy in around:
+        copy.start()
+    own_h = pltpu.make_async_copy(g4, g32.at[place.d], local_sem.at[1])
+    own_h.start()
+    for way in (0, 1):
+        gate_ring.advance(way, 0)
+    own_h.wait()
+    for k in range(1, n):
+        slot = g32.at[lax.rem(place.d + n - k, n)]
+        remote(g4, slot, h_send.at[k], h_recv.at[k], {"dp": place.right}).wait_recv()
+    pieces = g32[...].reshape(-1, 128).astype(BF16)
+    wide = matmul(pieces, spread_ref[...])
+    inside, kind = gain_lanes(n, wide.shape)
+    gain = jnp.sum(jnp.where(inside & (kind == 0), wide, 0.0), axis=0, keepdims=True)
+    gain_two = jnp.sum(jnp.where(inside & (kind == 1), wide, 0.0), axis=0, keepdims=True)
+    gains_ref[...] = jnp.concatenate([gain, gain_two] + [jnp.zeros_like(gain)] * 6, axis=0)
+    nfull[rows, :] = (x_ref[...] * scale * gain).astype(BF16)
+    pair = PairGather(place, nfull, pair_send, pair_recv)
+    cots = PairGather(place, cfull, cot_send, cot_recv)
+    for chunk in range(2):
+        pair.begin(chunk)
+    for chunk in range(2):
+        cots.begin(chunk)
+    bias_tiles(line_ref, tiles_ref)
+    for step in (1, 2):
+        for way in (0, 1):
+            ring.advance(way, step)
+        if step == 1:
+            pair.relay(0)
+        for way in (0, 1):
+            gate_ring.advance(way, step)
+    pair.relay(1)
+    for way in (0, 1):
+        ring.advance(way, 3)
+    for chunk in range(2):
+        pair.end(chunk)
+    out_n = pltpu.make_async_copy(nfull, normed_out, local_sem.at[2])
+    out_n.start()
+    for step in range(4, n // 2 + 1):
+        for way in (0, 1):
+            ring.advance(way, step)
+    for way in (0, 1):
+        gate_ring.advance(way, 3)
+    cots.relay(0)
+    width = qkv_ref.shape[1]
+    wqkv_ref[...] = wfull[:, :, :width]
+    wmix_ref[...] = wfull[:, :, width:]
+    weight = wqkv_ref[...].reshape(-1, width)
+
+    @pl.loop(0, 4)
+    def _(block):
+        rows = pl.ds(pl.multiple_of(block * size, size), size)
+        qkv_ref[rows, :] = matmul(nfull[rows, :], weight).astype(BF16)
+
+    cots.relay(1)
+    for step in range(4, n // 2 + 1):
+        for way in (0, 1):
+            gate_ring.advance(way, step)
+    out_g = pltpu.make_async_copy(gfull, wgate_out, local_sem.at[0])
+    out_g.start()
+    for chunk in range(2):
+        cots.end(chunk)
+    out_c = pltpu.make_async_copy(cfull, cot_out, local_sem.at[1])
+    out_c.start()
+    ring.finish()
+    gate_ring.finish()
+    for copy in small + around:
+        copy.wait_send()
+    out_n.wait()
+    out_g.wait()
+    out_c.wait()
+
+
+def enter(n, x, cot, gain, spread, weights, wgate, lines, kinds=5):
+    size, features = x.shape
+    rows, columns = weights.shape
+    wide = wgate.shape[1]
+    heads = columns // 4
+    count = (lines.shape[0] - 1) // kinds
+    block = lines.shape[1] // 2
+    return pl.pallas_call(
+        functools.partial(enter_kernel, n),
+        name="enter",
+        out_shape=(
+            jax.ShapeDtypeStruct((4 * size, features), BF16),
+            jax.ShapeDtypeStruct((4 * size, features), BF16),
+            jax.ShapeDtypeStruct((n, rows, wide), BF16),
+            jax.ShapeDtypeStruct((4 * size, 3 * heads), BF16),
+            jax.ShapeDtypeStruct((n, rows, 3 * heads), BF16),
+            jax.ShapeDtypeStruct((n, rows, heads), BF16),
+            jax.ShapeDtypeStruct((8, features), F32),
+            jax.ShapeDtypeStruct((count, kinds, block, block), F32),
+        ),
+        in_specs=[VMEM_SPEC] * 7,
+        out_specs=(ANY_SPEC,) * 3 + (VMEM_SPEC,) * 5,
+        scratch_shapes=[
+            pltpu.VMEM((n, rows, columns), BF16),
+            pltpu.VMEM((n, rows, wide), BF16),
+            pltpu.VMEM((4 * size, features), BF16),
+            pltpu.VMEM((4 * size, features), BF16),
+            pltpu.VMEM((4, 8, 128), F32),
+            pltpu.VMEM((n, 4, 8, 128), F32),
+            DMA((2, n // 2)), DMA((2, n // 2)),
+            DMA((2, n // 2)), DMA((2, n // 2)),
+            DMA((3, 2)), DMA((3, 2)),
+            DMA((3, 2)), DMA((3, 2)),
+            DMA((4,)), DMA((4,)),
+            DMA((n,)), DMA((n,)),
+            DMA((3,)),
+        ],
+        compiler_params=pltpu.CompilerParams(collective_id=0, has_side_effects=True),
+    )(x, cot, gain, spread, weights, wgate, lines)
+
+
+def middle_kernel(
+    n, ctx_ref, wmix_ref, x_ref, gains_ref, wlift_ref, wdown_ref, wgate_any,
+    second_out, lift_out, down_out, bend_out, slope_out, hidden_out, middle_ref,
+    lfull, dfull, gate_v, sfull, own_v, bend_v, slope_v, hidden_v,
+    give, got, over, came, sc_send, sc_recv,
+    pair_send, pair_recv, lift_send, lift_recv, down_send, down_recv, local_sem, out_sem,
+):
+    place = Place(n)
+    size = x_ref.shape[0]
+    own_l = pltpu.make_async_copy(wlift_ref, lfull.at[place.d], local_sem.at[0])
+    own_d = pltpu.make_async_copy(wdown_ref, dfull.at[place.d], local_sem.at[1])
+    load_g = pltpu.make_async_copy(wgate_any, gate_v, local_sem.at[2])
+    for copy in (own_l, own_d, load_g):
+        copy.start()
+    place.barrier()
+    lift = RingGather(place, lfull, lift_send, lift_recv)
+    down = RingGather(place, dfull, down_send, down_recv)
+    scatter = PairScatter(place, give, got, over, came, sc_send, sc_recv)
+    pair = PairGather(place, sfull, pair_send, pair_recv)
+    own_l.wait()
+    own_d.wait()
+
+    def both(ring, step):
+        for way in (0, 1):
+            ring.advance(way, step)
+
+    both(lift, 0)
+    weight = wmix_ref[...].reshape(-1, wmix_ref.shape[2])
+
+    def part(owner):
+        return matmul_nt(ctx_ref[block_rows(place, owner, size), :], weight)
+
+    scatter.far(part(place.far))
+    scatter.twin(part(place.twin))
+    scatter.mate(part(place.mate))
+    own_v[...] = part(place.m)
+    both(down, 0)
+    both(lift, 1)
+    gain = gains_ref[1:2, :]
+    chunk_rows = size // 2
+    for chunk in range(2):
+        rows = slice(chunk * chunk_rows, (chunk + 1) * chunk_rows)
+        middle = x_ref[rows, :] + scatter.take(chunk, own_v[rows, :])
+        middle_ref[rows, :] = middle
+        start = pl.multiple_of(place.m * size + chunk * chunk_rows, chunk_rows)
+        sfull[pl.ds(start, chunk_rows), :] = (middle * norm_scale(middle) * gain).astype(BF16)
+        pair.begin(chunk)
+    load_g.wait()
+
+    def gate_block(owner):
+        rows = block_rows(place, owner, size)
+        gate = matmul(sfull[rows, :], gate_v[...].reshape(-1, gate_v.shape[2]))
+        bend, slope = gate_terms(gate)
+        bend_v[rows, :] = bend
+        slope_v[rows, :] = slope
+
+    gate_block(place.m)
+    both(down, 1)
+    both(lift, 2)
+    pair.relay(0)
+    pair.relay(1)
+    both(down, 2)
+    both(lift, 3)
+    for chunk in range(2):
+        pair.end(chunk)
+    out_s = pltpu.make_async_copy(sfull, second_out, local_sem.at[0])
+    out_s.start()
+
+    @pl.loop(1, 4)
+    def _(k):
+        gate_block(lax.rem(place.m + k, 4))
+
+    both(lift, 4)
+    out_b = pltpu.make_async_copy(bend_v, bend_out, local_sem.at[1])
+    out_b.start()
+    out_l = pltpu.make_async_copy(lfull, lift_out, local_sem.at[2])
+    out_l.start()
+    both(down, 3)
+
+    @pl.loop(0, 4)
+    def _(k):
+        rows = pl.ds(pl.multiple_of(k * size, size), size)
+        lifted = matmul(sfull[rows, :], lfull[...].reshape(-1, lfull.shape[2]))
+        hidden_v[rows, :] = (bend_v[rows, :] * lifted).astype(BF16)
+        slope_v[rows, :] = slope_v[rows, :] * lifted
+
+    out_p = pltpu.make_async_copy(slope_v, slope_out, out_sem.at[0])
+    out_h = pltpu.make_async_copy(hidden_v, hidden_out, out_sem.at[1])
+    out_d = pltpu.make_async_copy(dfull, down_out, out_sem.at[2])
+    out_p.start()
+    out_h.start()
+    both(down, 4)
+    out_d.start()
+    lift.finish()
+    down.finish()
+    scatter.finish()
+    for copy in (out_s, out_b, out_l, out_p, out_h, out_d):
+        copy.wait()
+
+
+def middle_part(n, ctx, wmix, x, gains, wlift, wdown, wgate):
+    size, features = x.shape
+    rows, wide = wlift.shape
+    length = 4 * size
+    full = jax.ShapeDtypeStruct((n, rows, wide), BF16)
+    return pl.pallas_call(
+        functools.partial(middle_kernel, n),
+        name="middle",
+        out_shape=(
+            jax.ShapeDtypeStruct((length, features), BF16),
+            full,
+            full,
+            jax.ShapeDtypeStruct((length, wide), F32),
+            jax.ShapeDtypeStruct((length, wide), F32),
+            jax.ShapeDtypeStruct((length, wide), BF16),
+            jax.ShapeDtypeStruct((size, features), F32),
+        ),
+        in_specs=[VMEM_SPEC] * 6 + [ANY_SPEC],
+        out_specs=(ANY_SPEC,) * 6 + (VMEM_SPEC,),
+        scratch_shapes=[
+            pltpu.VMEM((n, rows, wide), BF16),
+            pltpu.VMEM((n, rows, wide), BF16),
+            pltpu.VMEM((n, rows, wide), BF16),
+            pltpu.VMEM((length, features), BF16),
+            pltpu.VMEM((size, features), F32),
+            pltpu.VMEM((length, wide), F32),
+            pltpu.VMEM((length, wide), F32),
+            pltpu.VMEM((length, wide), BF16),
+            *PairScatter.scratch(size, features),
+            DMA((3, 2)), DMA((3, 2)),
+            DMA((2, n // 2)), DMA((2, n // 2)),
+            DMA((2, n // 2)), DMA((2, n // 2)),
+            DMA((3,)), DMA((3,)),
+        ],
+        compiler_params=pltpu.CompilerParams(collective_id=1, has_side_effects=True),
+    )(ctx, wmix, x, gains, wlift, wdown, wgate)
+
+
+def norm_back(values, gain, grad):
+    scale = norm_scale(values)
+    term = grad * values
+    inner = jnp.mean(term * gain, axis=-1, keepdims=True)
+    return gain * scale * grad - values * (scale * scale * scale * inner), term * scale
+
+
+def back_kernel(
+    n, middle_ref, cotangent_ref, gains_ref, hidden_any, cot_any, second_any, bend_any, slope_any, wgate_any, wlift_any, wdown_any,
+    mixed_out, middle_cot_ref, feed_ref, grad_down_ref, grad_gate_ref, grad_lift_ref,
+    hidden_v, cot_v, second_v, gate_v, lift_v, down_v, bend_v, slope_v, gcot_v, lcot_v, mixed_v, own_v,
+    give, got, over, came, sc_send, sc_recv,
+    pair_send, pair_recv,
+    put_d, in_d, send_d, recv_d, put_g, in_g, send_g, recv_g, put_l, in_l, send_l, recv_l,
+    load_sem, piece_sem, out_sem,
+):
+    place = Place(n)
+    size = middle_ref.shape[0]
+    loads = [
+        pltpu.make_async_copy(source, target, load_sem.at[k])
+        for k, (source, target) in enumerate(
+            ((hidden_any, hidden_v), (cot_any, cot_v), (wdown_any, down_v), (wgate_any, gate_v), (wlift_any, lift_v), (second_any, second_v))
+        )
+    ]
+    for copy in loads:
+        copy.start()
+    order = (place.far, place.twin, place.mate, place.m)
+
+    def pieces(k):
+        rows = block_rows(place, order[k], size)
+        return [
+            pltpu.make_async_copy(source.at[rows], target.at[k % 2], piece_sem.at[k % 2, i])
+            for i, (source, target) in enumerate(((bend_any, bend_v), (slope_any, slope_v)))
+        ]
+
+    for copy in pieces(0):
+        copy.start()
+    place.barrier()
+    down = RingScatter(place, lambda slot: matmul_tn(slot_columns(cot_v, slot, n), hidden_v[...]), grad_down_ref, put_d, in_d, send_d, recv_d)
+    gate = RingScatter(place, lambda slot: matmul_tn(slot_columns(second_v, slot, n), gcot_v[...]), grad_gate_ref, put_g, in_g, send_g, recv_g)
+    lift = RingScatter(place, lambda slot: matmul_tn(slot_columns(second_v, slot, n), lcot_v[...]), grad_lift_ref, put_l, in_l, send_l, recv_l)
+    scatter = PairScatter(place, give, got, over, came, sc_send, sc_recv)
+    pair = PairGather(place, mixed_v, pair_send, pair_recv)
+
+    def both(ring, step):
+        for way in (0, 1):
+            ring.advance(way, step)
+
+    def flat(ref):
+        return ref[...].reshape(-1, ref.shape[2])
+
+    loads[0].wait()
+    loads[1].wait()
+    both(down, 0)
+    for copy in loads[2:5]:
+        copy.wait()
+    for k in range(4):
+        rows = block_rows(place, order[k], size)
+        if k < 3:
+            for copy in pieces(k + 1):
+                copy.start()
+        hidden_cot = matmul(cot_v[rows, :], flat(down_v))
+        for copy in pieces(k):
+            copy.wait()
+        gate_cot = (hidden_cot * slope_v[k % 2]).astype(BF16)
+        lift_cot = (hidden_cot * bend_v[k % 2]).astype(BF16)
+        gcot_v[rows, :] = gate_cot
+        lcot_v[rows, :] = lift_cot
+        part = matmul_nt(gate_cot, flat(gate_v)) + matmul_nt(lift_cot, flat(lift_v))
+        if k == 0:
+            scatter.far(part)
+        elif k == 1:
+            scatter.twin(part)
+            both(down, 1)
+        elif k == 2:
+            scatter.mate(part)
+        else:
+            own_v[...] = part
+    loads[5].wait()
+    both(gate, 0)
+    both(down, 2)
+    both(lift, 0)
+    chunk_rows = size // 2
+    gain = gains_ref[1:2, :]
+    feed = jnp.zeros_like(gain)
+    for chunk in range(2):
+        rows = slice(chunk * chunk_rows, (chunk + 1) * chunk_rows)
+        grad = scatter.take(chunk, own_v[rows, :])
+        through, term = norm_back(middle_ref[rows, :], gain, grad)
+        middle_cot = cotangent_ref[rows, :] + through
+        middle_cot_ref[rows, :] = middle_cot
+        feed += jnp.sum(term, axis=0, keepdims=True)
+        start = pl.multiple_of(place.m * size + chunk * chunk_rows, chunk_rows)
+        mixed_v[pl.ds(start, chunk_rows), :] = middle_cot.astype(BF16)
+        pair.begin(chunk)
+    feed_ref[...] = jnp.concatenate([feed] + [jnp.zeros_like(feed)] * 7, axis=0)
+    scatter.finish()
+    both(gate, 1)
+    both(down, 3)
+    both(lift, 1)
+    pair.relay(0)
+    pair.relay(1)
+    both(gate, 2)
+    down.finish()
+    both(lift, 2)
+    for chunk in range(2):
+        pair.end(chunk)
+    out_m = pltpu.make_async_copy(mixed_v, mixed_out, out_sem.at[0])
+    out_m.start()
+    both(gate, 3)
+    both(lift, 3)
+    gate.finish()
+    lift.finish()
+    out_m.wait()
+
+
+def back_part(n, middle, cotangent, gains, hidden, cot, second, bend, slope, wgate, wlift, wdown):
+    size, features = middle.shape
+    length, wide = hidden.shape
+    rows = wgate.shape[1]
+    grad = jax.ShapeDtypeStruct((rows, wide), F32)
+    weight = pltpu.VMEM((n, rows, wide), BF16)
+    return pl.pallas_call(
+        functools.partial(back_kernel, n),
+        name="back",
+        out_shape=(
+            jax.ShapeDtypeStruct((length, features), BF16),
+            jax.ShapeDtypeStruct((size, features), F32),
+            jax.ShapeDtypeStruct((8, features), F32),
+            grad, grad, grad,
+        ),
+        in_specs=[VMEM_SPEC] * 3 + [ANY_SPEC] * 8,
+        out_specs=(ANY_SPEC,) + (VMEM_SPEC,) * 5,
+        scratch_shapes=[
+            pltpu.VMEM((length, wide), BF16),
+            pltpu.VMEM((length, features), BF16),
+            pltpu.VMEM((length, features), BF16),
+            weight, weight, weight,
+            pltpu.VMEM((2, size, wide), F32),
+            pltpu.VMEM((2, size, wide), F32),
+            pltpu.VMEM((length, wide), BF16),
+            pltpu.VMEM((length, wide), BF16),
+            pltpu.VMEM((length, features), BF16),
+            pltpu.VMEM((size, features), F32),
+            *PairScatter.scratch(size, features),
+            DMA((3, 2)), DMA((3, 2)),
+            *RingScatter.scratch(n, rows, wide),
+            *RingScatter.scratch(n, rows, wide),
+            *RingScatter.scratch(n, rows, wide),
+            DMA((6,)), DMA((2, 2)), DMA((1,)),
+        ],
+        compiler_params=pltpu.CompilerParams(collective_id=2, has_side_effects=True, vmem_limit_bytes=67043328),
+    )(middle, cotangent, gains, hidden, cot, second, bend, slope, wgate, wlift, wdown)
+
+
+def leave_kernel(
+    n, cots_ref, ctx_ref, wqkv_ref, x_ref, gains_ref, middle_cot_ref, feed_ref, table_ref, spread_ref,
+    middle_ref, hidden_ref, normed_any, mixed_any, wdown_any,
+    grad_ref, gain_out, table_out, input_ref, output_ref,
+    normed_v, mixed_v, down_v, own_v, own_two,
+    give, got, over, came, sc_send, sc_recv,
+    give_two, got_two, over_two, came_two, sd_send, sd_recv,
+    put, inbox, ring_send, ring_recv,
+    tables, pieces_v, spare_v, sum_v, last_v,
+    t_send, t_recv, g_send, g_recv, h_send, h_recv, load_sem,
+):
+    place = Place(n)
+    size = x_ref.shape[0]
+    load_n = pltpu.make_async_copy(normed_any, normed_v, load_sem.at[0])
+    load_m = pltpu.make_async_copy(mixed_any, mixed_v, load_sem.at[1])
+    load_d = pltpu.make_async_copy(wdown_any, down_v, load_sem.at[2])
+    for copy in (load_n, load_m, load_d):
+        copy.start()
+    place.barrier(everyone=True)
+
+    def peer(k):
+        return {"dp": lax.rem(place.d + k, n)}
+
+    table_copies = [remote(table_ref, tables.at[n - k], t_send.at[k], t_recv.at[k], peer(k)) for k in range(1, n)]
+    for copy in table_copies:
+        copy.start()
+    scatter = PairScatter(place, give, got, over, came, sc_send, sc_recv)
+    downs = PairScatter(place, give_two, got_two, over_two, came_two, sd_send, sd_recv)
+
+    def term(slot):
+        left = matmul_tn(slot_columns(normed_v, slot, n), cots_ref[...])
+        return jnp.concatenate([left, matmul_tn(slot_columns(mixed_v, slot, n), ctx_ref[...])], axis=1)
+
+    ring = RingScatter(place, term, grad_ref, put, inbox, ring_send, ring_recv)
+
+    def both(step):
+        for way in (0, 1):
+            ring.advance(way, step)
+
+    def part(owner):
+        weight = wqkv_ref[...].reshape(-1, wqkv_ref.shape[2])
+        return matmul_nt(cots_ref[block_rows(place, owner, size), :], weight)
+
+    def part_two(owner):
+        weight = down_v[...].reshape(-1, down_v.shape[2])
+        return matmul_nt(hidden_ref[block_rows(place, owner, size), :], weight)
+
+    scatter.far(part(place.far))
+    scatter.twin(part(place.twin))
+    load_n.wait()
+    load_m.wait()
+    both(0)
+    scatter.mate(part(place.mate))
+    own_v[...] = part(place.m)
+    load_d.wait()
+    downs.far(part_two(place.far))
+    downs.twin(part_two(place.twin))
+    both(1)
+    downs.mate(part_two(place.mate))
+    own_two[...] = part_two(place.m)
+    both(2)
+    chunk_rows = size // 2
+    gain = gains_ref[0:1, :]
+    total = jnp.zeros_like(gain)
+    for chunk in range(2):
+        rows = slice(chunk * chunk_rows, (chunk + 1) * chunk_rows)
+        grad = scatter.take(chunk, own_v[rows, :])
+        through, terms = norm_back(x_ref[rows, :], gain, grad)
+        input_ref[rows, :] = middle_cot_ref[rows, :] + through
+        total += jnp.sum(terms, axis=0, keepdims=True)
+    inside, kind = gain_lanes(n, (n * 4 * 8, gain.shape[1]))
+    rows = jnp.where(inside & (kind == 0), total, 0.0) + jnp.where(inside & (kind == 1), feed_ref[0:1, :], 0.0)
+    rows = lax.dot_general(
+        rows, spread_ref[...].astype(F32), (((1,), (1,)), ((), ())), precision=lax.Precision.HIGHEST, preferred_element_type=F32
+    )
+    pieces_v[...] = rows.reshape(pieces_v.shape)
+    around = [remote(pieces_v.at[lax.rem(place.d + k, n)], spare_v.at[n - k], g_send.at[k], g_recv.at[k], peer(k)) for k in range(1, n)]
+    for copy in around:
+        copy.start()
+    both(3)
+    table = table_ref[...]
+    for k in range(1, n):
+        remote(table_ref, tables.at[n - k], t_send.at[k], t_recv.at[k], peer(k)).wait_recv()
+        table += tables[n - k]
+    table_out[...] = table
+    sums = pieces_v[place.d]
+    for k in range(1, n):
+        remote(pieces_v.at[0], spare_v.at[n - k], g_send.at[k], g_recv.at[k], peer(k)).wait_recv()
+        sums += spare_v[n - k]
+    sum_v[...] = sums
+    last = []
+    for k in range(1, 4):
+        target = lax.rem(place.m + k, 4)
+        last.append(remote(sum_v.at[target], last_v.at[4 - k], h_send.at[k], h_recv.at[k], {"mp": target}))
+        last[-1].start()
+    for chunk in range(2):
+        rows = slice(chunk * chunk_rows, (chunk + 1) * chunk_rows)
+        output_ref[rows, :] = middle_ref[rows, :] + downs.take(chunk, own_two[rows, :])
+    ring.finish()
+    sums = sum_v[place.m]
+    for k in range(1, 4):
+        remote(sum_v.at[0], last_v.at[4 - k], h_send.at[k], h_recv.at[k], {"mp": place.mate}).wait_recv()
+        sums += last_v[4 - k]
+    gain_out[...] = sums
+    scatter.finish()
+    downs.finish()
+    for copy in table_copies + around + last:
+        copy.wait_send()
+
+
+def leave_part(n, cots, ctx, wqkv, x, gains, middle_cot, feed, table, spread, middle, hidden, normed, mixed, wdown):
+    size, features = x.shape
+    length, width = cots.shape
+    rows = wqkv.shape[1]
+    columns = width + ctx.shape[1]
+    return pl.pallas_call(
+        functools.partial(leave_kernel, n),
+        name="leave",
+        out_shape=(
+            jax.ShapeDtypeStruct((rows, columns), F32),
+            jax.ShapeDtypeStruct((8, 128), F32),
+            jax.ShapeDtypeStruct((8, 128), F32),
+            jax.ShapeDtypeStruct((size, features), F32),
+            jax.ShapeDtypeStruct((size, features), F32),
+        ),
+        in_specs=[VMEM_SPEC] * 11 + [ANY_SPEC] * 3,
+        out_specs=(VMEM_SPEC,) * 5,
+        scratch_shapes=[
+            pltpu.VMEM((length, features), BF16),
+            pltpu.VMEM((length, features), BF16),
+            pltpu.VMEM(wdown.shape, BF16),
+            pltpu.VMEM((size, features), F32),
+            pltpu.VMEM((size, features), F32),
+            *PairScatter.scratch(size, features),
+            *PairScatter.scratch(size, features),
+            *RingScatter.scratch(n, rows, columns),
+            pltpu.VMEM((n, 8, 128), F32),
+            pltpu.VMEM((n, 4, 8, 128), F32),
+            pltpu.VMEM((n, 4, 8, 128), F32),
+            pltpu.VMEM((4, 8, 128), F32),
+            pltpu.VMEM((4, 8, 128), F32),
+            DMA((n,)), DMA((n,)),
+            DMA((n,)), DMA((n,)),
+            DMA((4,)), DMA((4,)),
+            DMA((3,)),
+        ],
+        compiler_params=pltpu.CompilerParams(collective_id=3, has_side_effects=True),
+    )(cots, ctx, wqkv, x, gains, middle_cot, feed, table, spread, middle, hidden, normed, mixed, wdown)
+
+
 THRESHOLDS = (8, 12, 16, 23, 32, 46, 64, 91)
 HIGHEST = lax.Precision.HIGHEST
 MASKED = -1e30
@@ -84,7 +1144,7 @@
     return result
 
 
-def local(
+def native(
     inputs,
     segments,
     attend_gain,
@@ -266,7 +1326,91 @@
     )
 
 
+BLOCK = 256
+KINDS = 5
+
+
+def tile_buckets(block):
+    column = jnp.arange(2 * block)
+    column = jnp.where(column < block, column, column - 2 * block)
+    kind = jnp.arange(KINDS)[:, None]
+    offset = column[None, :] + (kind - 2) * block
+    offset = jnp.where(kind == 0, -2 * block, jnp.where(kind == KINDS - 1, 2 * block, offset))
+    distance = jnp.abs(offset)
+    far_bucket = 7 + sum(((distance >= limit).astype(jnp.int32) for limit in THRESHOLDS))
+    return jnp.where(distance < 8, distance, far_bucket) + jnp.where(offset > 0, 16, 0)
+
+
+def fused(
+    n,
+    inputs,
+    segments,
+    attend_gain,
+    feed_gain,
+    w_query,
+    w_key,
+    w_value,
+    w_mixer,
+    rel_table,
+    w_gate,
+    w_lift,
+    w_down,
+    cotangent,
+):
+    x, cot = inputs[0], cotangent[0]
+    size = x.shape[0]
+    hidden_here = w_gate.shape[1]
+    heads = rel_table.shape[1]
+    head_width = w_query.shape[1]
+    per = attend_gain.shape[0]
+    spare = -hidden_here % 128
+    gain = jnp.pad(jnp.stack([attend_gain, feed_gain]), ((0, 6), (0, 128 - per)))
+    spread_rows = (jnp.arange(x.shape[1])[None, :] % per == jnp.arange(128)[:, None]).astype(BF16)
+    attention = jnp.concatenate([w_query, w_key, w_value, w_mixer.T], axis=1).astype(BF16)
+    wgate, wlift, wdown = (
+        jnp.pad(part.astype(BF16), ((0, 0), (0, spare))) for part in (w_gate, w_lift, w_down.T)
+    )
+    onehot = (tile_buckets(BLOCK)[..., None] == jnp.arange(128)).astype(F32)
+    count = rel_table.shape[0]
+    lines = jnp.einsum("tkb,bh->htk", onehot[..., :count], rel_table, precision=HIGHEST)
+    lines = jnp.pad(lines.reshape(heads * KINDS, -1), ((0, 1), (0, 0)))
+
+    normed, cots, gate_full, qkv, wqkv, wmix, gains, tiles = enter(
+        n, x, cot, gain, spread_rows, attention, wgate, lines
+    )
+    context, context32, logsum = attend(qkv, segments, tiles)
+    second, lift_full, down_full, bend, slope, hidden, middle = middle_part(
+        n, context, wmix, x, gains, wlift, wdown, gate_full
+    )
+    mixed, middle_cot, feed, down_term, gate_term, lift_term = back_part(
+        n, middle, cot, gains, hidden, cots, second, bend, slope, gate_full, lift_full, down_full
+    )
+    qkv_cot, table = attend_back(qkv, segments, tiles, context32, logsum, mixed, wmix, onehot)
+    attention_term, gain_term, table_term, input_grad, output = leave_part(
+        n, qkv_cot, context, wqkv, x, gains, middle_cot, feed, table, spread_rows, middle, hidden, normed, mixed, down_full
+    )
+    return (
+        output[None],
+        input_grad[None],
+        gain_term[0, :per],
+        gain_term[1, :per],
+        attention_term[:, :head_width],
+        attention_term[:, head_width : 2 * head_width],
+        attention_term[:, 2 * head_width : 3 * head_width],
+        attention_term[:, 3 * head_width :].T,
+        table_term[:heads, :count].T,
+        gate_term[:, :hidden_here],
+        lift_term[:, :hidden_here],
+        down_term[:, :hidden_here].T,
+    )
+
+
+def kernels_fit(mesh):
+    return mesh.shape["dp"] == 8 and mesh.shape["mp"] == 4
+
+
 def solution(mesh):
+    local = functools.partial(fused, mesh.shape["dp"]) if kernels_fit(mesh) else native
     return jax.shard_map(
         local,
         mesh=mesh,

time: 1430 us -> 392 us (0.27)
  waiting for transfers between devices: 809 us -> 0 us
  Pallas kernels: 0 us -> 364 us
  matrix products: 263 us -> 0.65 us
  blocking collectives: 232 us -> 0 us
  local copies, waits for them, and re-layouts: 55.5 us -> 16.2 us
  other arithmetic: 45.5 us -> 7.45 us
  between operations: 16.4 us -> 1 us
    reduce_scatter x10 -> x0, waiting for transfers between devices: 619 us -> none  [the longest x4 163 us: spread(): return lax.psum_scatter(part, 'mp', scatter_dimension=1, tiled=True)]
    pallas_call x0 -> x6, Pallas kernels: none -> 364 us  [the longest x1 104 us: back_part(): pl.pallas_call(functools.partial(back_kernel, n), name='back', out_shape=...]
    dot_general x42 -> x1, matrix products: 259 us -> 0.65 us  [fused(): jnp.einsum('tkb,bh->htk', onehot[..., :count], rel_table, precision=HIGHEST)]
    all_gather x7 -> x0, waiting for transfers between devices: 189 us -> none  [the longest x4 72.7 us: collect(): return lax.all_gather(part, 'mp', axis=1, tiled=True)]
    all_gather x4 -> x0, blocking collectives: 128 us -> none  [the longest x1 32.3 us: local(): lax.all_gather(w_query.astype(jnp.bfloat16), 'dp', axis=0, tiled=True)]
    unnamed x2 -> x0, blocking collectives: 80.7 us -> none
    transpose x2 -> x3, local copies, waits for them, and re-layouts: 29.1 us -> 3.1 us  [the longest x1 1.26 us: fused(): table_term[:heads, :count]]
    psum x1 -> x0, blocking collectives: 22.7 us -> none  [local(): lax.psum(table_terms(score_total, buckets, rel_table.shape[0]), 'dp')]
  transfers between devices with their start and end apart: 18 -> 0, of which waited for: 14 -> 0; matrix products, arithmetic and copies ran while one was open for 21% -> 0% of each run, Pallas kernels for 0% -> 0%
where the time goes in v1:
time: 392 us; the launch traced here: 389 us
  Pallas kernels  364 us (93%)
  local copies, waits for them, and re-layouts  16.2 us (4%)
  other arithmetic  7.45 us (2%)
    pallas_call x1, Pallas kernels, back_part(): pl.pallas_call(functools.partial(back_kernel, n), name='back', out_shape=...  104 us
    pallas_call x1, Pallas kernels, middle_part(): pl.pallas_call(functools.partial(middle_kernel, n), name='middle', out_sh...  82.2 us
    pallas_call x1, Pallas kernels, enter(): pl.pallas_call(functools.partial(enter_kernel, n), name='enter', out_shap...  71 us
    pallas_call x1, Pallas kernels, leave_part(): pl.pallas_call(functools.partial(leave_kernel, n), name='leave', out_shap...  49 us
    pallas_call x1, Pallas kernels, attend_back(): pl.pallas_call(attend_back_kernel, name='attend_back', out_shape=(jax.Sha...  46.1 us
    pallas_call x1, Pallas kernels, attend(): pl.pallas_call(attend_kernel, name='attend', out_shape=(jax.ShapeDtypeStr...  11.8 us

profile of v1, /device:TPU:0, one launch (start us, length us, event | category | flops | bytes accessed | tf_op | source)
XLA Modules:
  0.0 389.4 jit_solution(16529710361580428980)
XLA Ops:
  0.6 0.0 copy-start.3
  0.7 1.3 select_maximum_fusion.gain_ref
  2.0 0.1 fusion.6
  2.1 0.9 convert.13
  3.1 0.9 convert.14
  4.0 0.9 convert.15
  5.0 1.0 copy.29
  6.0 0.0 copy-start.4
  6.0 0.9 pad_maximum_fusion.w_ref
  6.9 0.8 fusion.5.spread_ref
  7.7 0.0 copy-done.3
  7.8 0.0 copy-start.5
  7.8 0.8 pad.19.wgate_ref
  8.6 0.0 copy-done.4
  8.6 0.0 copy-start.9
  8.6 0.8 pad.21.wlift_ref
  9.4 0.0 copy-done.5
  9.5 0.0 copy-start.10
  9.5 0.8 pad.22.wdown_ref
  10.3 0.0 copy-done.9
  10.3 1.0 copy.33.segc_ref
  11.3 1.3 fusion.21
  12.6 0.0 copy-done.10
  12.6 0.6 fusion.2
  13.3 0.6 pad.20.line_ref
  14.0 71.0 %enter.1 = (bf16[1024,1536]{1,0:T(8,128)(2,1)}, bf16[1024,1536]{1,0:T(8,128)(2,1)}, bf16[8,192,1024]{2,1,0:T(8,128)(2,1)}, bf16[1024,576]{1,0:T(8,128)(2,1)}, bf...) custom-call(f32[256,1536]{1,0:T(8,128)} %bitcast.29, ...), custom_call_target="tpu_custom_call" | custom-call | tf_op jit(solution)/shard_map/enter/pallas_call | solution.py:590
  85.0 11.8 %attend.1 = (bf16[1024,192]{1,0:T(8,128)(2,1)}, f32[1024,192]{1,0:T(8,128)}, f32[1024,8]{1,0:T(8,128)}) custom-call(s32[1,1024]{1,0:T(1,128)} %segr_ref.3, bf16[1024,576]{1,0:T(8,128)(2,1)} %get-tuple-element.43.qkv_ref, s32[1,1024]{1,0:T(1,128)} %segr_ref.3, s32[1024,1]{1,0:T(8,128)} %copy.33.segc_ref, f32[3,5,256,256]{3,2,1,0:T(8,128)} %get-tuple-element.44.tiles_ref), custom_call_target="tpu_custom_call" | custom-call | tf_op jit(solution)/shard_map/attend/pallas_call | solution.py:337
  96.8 82.2 %middle.1 = (bf16[1024,1536]{1,0:T(8,128)(2,1)}, bf16[8,192,1024]{2,1,0:T(8,128)(2,1)}, bf16[8,192,1024]{2,1,0:T(8,128)(2,1)}, f32[1024,1024]{1,0:T(8,128)}, f32...) custom-call(bf16[1024,192]{1,0:T(8,128)(2,1)} %get-tuple-element.47.ctx_ref, ...), custom_call_target="tpu_custom_call" | custom-call | tf_op jit(solution)/shard_map/middle/pallas_call | solution.py:729
  179.0 104.0 %back.1 = (bf16[1024,1536]{1,0:T(8,128)(2,1)}, f32[256,1536]{1,0:T(8,128)}, f32[8,1536]{1,0:T(8,128)}, f32[192,1024]{1,0:T(8,128)}, f32[192,1024]{1,0:T(8,128)}, /*index=5*/f32[192,1024]{1,0:T(8,128)}) custom-call(f32[256,1536]{1,0:T(8,128)} %get-tuple-element.51.middle_ref, f32[256,1536]{1,0:T(8,128)} %bitcast.33, f32[8,1536]{1,0:T(8,128)} %get-tuple-element.49.gains_ref, ...), custom_call_target="tpu_custom_call" | custom-call | tf_op jit(solution)/shard_map/back/pallas_call | solution.py:884
  283.0 46.1 %attend_back.1 = (bf16[1024,576]{1,0:T(8,128)(2,1)}, f32[8,128]{1,0:T(8,128)}) custom-call(s32[1,1024]{1,0:T(1,128)} %segr_ref.3, bf16[1024,576]{1,0:T(8,128)(2,1)} %get-tuple-element.43.qkv_ref, s32[1,1024]{1,0:T(1,128)} %segr_ref.3, s32[1024,1]{1,0:T(8,128)} %copy.33.segc_ref, f32[3,5,256,256]{3,2,1,0:T(8,128)} %get-tuple-element.44.tiles_ref, ...), custom_call_target="tpu_custom_call" | custom-call | tf_op jit(solution)/shard_map/attend_back/pallas_call | solution.py:441
  329.1 0.0 copy-start.8
  329.1 49.0 %leave.1 = (f32[192,768]{1,0:T(8,128)}, f32[8,128]{1,0:T(8,128)}, f32[8,128]{1,0:T(8,128)}, f32[256,1536]{1,0:T(8,128)}, f32[256,1536]{1,0:T(8,128)}) custom-call(bf16[1024,576]{1,0:T(8,128)(2,1)} %get-tuple-element.60.cots_ref, bf16[1024,192]{1,0:T(8,128)(2,1)} %get-tuple-element.47.ctx_ref, bf16[8,192,576]{2,1,0:T(8,128)(2,1)} %get-tuple-element.61.wqkv_ref, ...), custom_call_target="tpu_custom_call" | custom-call | tf_op jit(solution)/shard_map/leave/pallas_call | solution.py:1032
  378.1 0.0 copy-start.2
  378.1 1.3 slice_bitcast_fusion.3
  379.4 1.3 slice_bitcast_fusion.2
  380.6 0.0 copy-done.8
  380.6 0.0 copy-start.1
  380.6 0.9 slice_bitcast_fusion
  381.6 0.0 copy-done.2
  381.6 0.9 slice_bitcast_fusion.1
  382.5 0.8 copy.34
  383.3 0.0 copy-done.1
  383.3 0.0 copy-start
  383.3 1.1 copy.41
  384.4 0.8 copy-done
  385.2 0.0 copy-start.7
  385.3 1.1 copy.42
  386.4 0.5 copy-done.7
  386.9 0.0 copy-start.6
  386.9 0.9 copy.43
  387.8 0.5 copy-done.6
  388.3 0.9 copy.44
  (9 shorter events, 0.2 us)
Async XLA Ops:
  0.6 7.1 %copy-start.3 = (f32[192,992]{1,0:T(8,128)S(1)}, f32[192,992]{1,0:T(8,128)}, u32[]{:S(2)}) copy-start(f32[192,992]{1,0:T(8,128)} %param.22) | copy-start | bytes 2285572
  6.0 2.6 copy-start.4
  7.8 1.7 copy-start.5
  8.6 1.7 copy-start.9
  9.5 3.2 copy-start.10
  329.1 51.5 %copy-start.8 = (f32[192,1024]{1,0:T(8,128)S(1)}, f32[192,1024]{1,0:T(8,128)}, u32[]{:S(2)}) copy-start(f32[192,1024]{1,0:T(8,128)} %get-tuple-element.73) | copy-start | bytes 2359300
  378.1 3.5 copy-start.2
  380.6 2.6 copy-start.1
  383.3 2.0 copy-start
  385.2 1.7 copy-start.7
  386.9 1.4 copy-start.6

commit v2 on v1

--- a/solution.py
+++ b/solution.py
@@ -8,6 +8,11 @@
 from jax.sharding import PartitionSpec as P
 
 EPSILON = 1e-06
+THRESHOLDS = (8, 12, 16, 23, 32, 46, 64, 91)
+HIGHEST = lax.Precision.HIGHEST
+MASKED = -1e30
+BLOCK = 256
+KINDS = 5
 MESH = pl.DeviceIdType.MESH
 BF16 = jnp.bfloat16
 F32 = jnp.float32
@@ -71,9 +76,9 @@
 
 
 class RingGather:
-    def __init__(self, place, full, send, recv):
+    def __init__(self, place, full, send, recv, first=0):
         self.place, self.full, self.send, self.recv = place, full, send, recv
-        self.steps = place.n // 2
+        self.steps, self.first = place.n // 2, first
 
     def part(self, way, position, step):
         slot = self.full.at[self.place.device(position + self.place.n)]
@@ -93,14 +98,14 @@
         return remote(ref, ref, self.send.at[way, step], self.recv.at[way, step], where)
 
     def advance(self, way, step):
-        if step:
+        if step > self.first:
             self.incoming(way, step - 1).wait_recv()
         if step < self.steps:
             self.outgoing(way, step).start()
 
     def finish(self):
         for way in (0, 1):
-            for step in range(self.steps):
+            for step in range(self.first, self.steps):
                 self.outgoing(way, step).wait_send()
 
 
@@ -129,8 +134,11 @@
     def end(self, chunk):
         self.copy(0, chunk, self.place.mate).wait_recv()
         self.copy(2, chunk, self.place.far).wait_recv()
-        for kind in range(3):
-            self.copy(kind, chunk, self.place.m).wait_send()
+
+    def finish(self):
+        for chunk in range(self.chunks):
+            for kind in range(3):
+                self.copy(kind, chunk, self.place.m).wait_send()
 
 
 def norm_scale(values):
@@ -195,8 +203,8 @@
 
 
 class RingScatter:
-    def __init__(self, place, term, out, put, inbox, send, recv):
-        self.place, self.term, self.out, self.put, self.inbox = place, term, out, put, inbox
+    def __init__(self, place, term, put, inbox, send, recv, last=None):
+        self.place, self.term, self.put, self.inbox, self.last = place, term, put, inbox, last
         self.send, self.recv = send, recv
         self.steps = place.n // 2
 
@@ -204,44 +212,55 @@
         source, target = self.put.at[way, step], self.inbox.at[way, step]
         if step == 0:
             half = source.shape[0] // 2
-            rows = pl.ds(half * way, half)
+            rows = pl.ds(pl.multiple_of(half * way, half), half)
             source, target = source.at[rows], target.at[rows]
-        where = {"dp": self.place.left if way else self.place.right}
+        where = {"dp": self.place.right + way * (self.place.left - self.place.right)}
         return remote(source, target, self.send.at[way, step], self.recv.at[way, step], where)
 
     def arrived(self, way, step, total):
         self.copy(way, step).wait_recv()
-        if step:
-            return total + self.inbox[way, step].astype(F32)
-        half = total.shape[0] // 2
-        if way:
-            return jnp.concatenate([total[:half], total[half:] + self.inbox[way, 0, half:, :].astype(F32)], axis=0)
-        return jnp.concatenate([total[:half] + self.inbox[way, 0, :half, :].astype(F32), total[half:]], axis=0)
-
-    def advance(self, way, step):
-        n = self.place.n
-        away = self.steps - step
-        owner = self.place.device(self.place.pos + (n - away if way else away))
-        total = self.term(owner)
-        if step:
-            total = self.arrived(way, step - 1, total)
-        self.put[way, step] = total.astype(BF16)
-        self.copy(way, step).start()
+        came = self.inbox[way, step].astype(F32)
+        if step == 0:
+            row = lax.broadcasted_iota(jnp.int32, came.shape, 0)
+            half = came.shape[0] // 2
+            came = jnp.where((row >= half * way) & (row < half * way + half), came, 0.0)
+        return total + came
+
+    def advance(self, step):
+        place, away = self.place, self.steps - step
+
+        @pl.loop(0, 2)
+        def _(way):
+            owner = place.device(place.pos + place.n + away * (1 - 2 * way))
+            total = self.term(owner)
+            if step:
+                total = self.arrived(way, step - 1, total)
+            if step == self.steps - 1 and self.last is not None:
+                self.copy(way, 0).wait_send()
+                self.put[way, 0] = total.astype(BF16)
+            else:
+                self.put[way, step] = total.astype(BF16)
+                self.copy(way, step).start()
+
+    def total(self):
+        total = self.term(self.place.d)
+        if self.last is None:
+            for way in (0, 1):
+                total = self.arrived(way, self.steps - 1, total)
+        return total
 
     def finish(self):
-        total = self.term(self.place.d)
+        handed = self.last is not None
         for way in (0, 1):
-            total = self.arrived(way, self.steps - 1, total)
-        self.out[...] = total
-        for way in (0, 1):
-            for step in range(self.steps):
+            for step in range(handed, self.steps - handed):
                 self.copy(way, step).wait_send()
 
     @staticmethod
-    def scratch(n, rows, columns):
+    def scratch(n, rows, columns, handed=False):
+        steps = n // 2 - handed
         return [
-            pltpu.VMEM((2, n // 2, rows, columns), BF16), pltpu.VMEM((2, n // 2, rows, columns), BF16),
-            DMA((2, n // 2)), DMA((2, n // 2)),
+            pltpu.VMEM((2, steps, rows, columns), BF16), pltpu.VMEM((2, steps, rows, columns), BF16),
+            DMA((2, steps)), DMA((2, steps)),
         ]
 
 
@@ -260,11 +279,26 @@
     return gate * half, slope
 
 
-def bias_tiles(row_ref, tiles_ref):
+def bucket_onehot(kind, block, count):
+    column = lax.broadcasted_iota(jnp.int32, (count, 2 * block), 1)
+    offset = jnp.where(column < block, column, column - 2 * block) + (kind - 2) * block
+    if kind in (0, KINDS - 1):
+        offset = jnp.full_like(column, (kind - 2) * block)
+    distance = jnp.abs(offset)
+    far_bucket = 7 + sum(((distance >= limit).astype(jnp.int32) for limit in THRESHOLDS))
+    bucket = jnp.where(distance < 8, distance, far_bucket) + jnp.where(offset > 0, 16, 0)
+    return (bucket == lax.broadcasted_iota(jnp.int32, bucket.shape, 0)).astype(F32)
+
+
+def bias_tiles(table_ref, tiles_ref):
     heads, kinds, block, _ = tiles_ref.shape
-    for h in range(heads):
-        for t in range(kinds):
-            line = jnp.broadcast_to(row_ref[pl.ds(h * kinds + t, 1), :], (block, 2 * block))
+    for t in range(kinds):
+        onehot = bucket_onehot(t, block, table_ref.shape[1])
+        lines = lax.dot_general(
+            table_ref[...], onehot, (((1,), (0,)), ((), ())), precision=HIGHEST, preferred_element_type=F32
+        )
+        for h in range(heads):
+            line = jnp.broadcast_to(lines[h : h + 1, :], (block, 2 * block))
             if t in (0, kinds - 1):
                 tiles_ref[h, t] = line[:, :block]
             else:
@@ -280,26 +314,35 @@
     return low, high - low
 
 
+def segment_column(segr_ref):
+    return jnp.broadcast_to(segr_ref[...].astype(F32), (8, segr_ref.shape[1])).T
+
+
+def window_blocks(segr_ref, segc_ref, rows, index, low, blocks, block):
+    places, sames, tile_at = [], [], []
+    for t in range(blocks):
+        j = low + t
+        place = pl.ds(pl.multiple_of(j * block, block), block)
+        places.append(place)
+        sames.append(segc_ref[rows, 0:1] == segr_ref[:, place].astype(F32))
+        tile_at.append(jnp.clip(j - index, -2, 2) + 2)
+    return places, sames, tile_at
+
+
 def score_block(query, key_rows, tile, same):
-    return jnp.where(same, matmul_nt(query, key_rows) + tile, -1e30)
-
-
-def attend_kernel(seg_smem, qkv_ref, segr_ref, segc_ref, tiles_ref, ctx_ref, ctx32_ref, lse_ref):
+    return jnp.where(same, matmul_nt(query, key_rows) + tile, MASKED)
+
+
+def attend_kernel(seg_smem, qkv_ref, segr_ref, tiles_ref, ctx_ref, ctx32_ref, lse_ref, segc_ref):
     heads, _, block, _ = tiles_ref.shape
     length, width = qkv_ref.shape
     width = width // (3 * heads)
     count = length // block
+    segc_ref[...] = segment_column(segr_ref)
 
     def run(index, low, blocks):
         rows = pl.ds(pl.multiple_of(index * block, block), block)
-        seg_q = segc_ref[rows, :]
-        places, sames, tile_at = [], [], []
-        for t in range(blocks):
-            j = low + t
-            place = pl.ds(pl.multiple_of(j * block, block), block)
-            places.append(place)
-            sames.append(seg_q == segr_ref[:, place])
-            tile_at.append(jnp.clip(j - index, -2, 2) + 2)
+        places, sames, tile_at = window_blocks(segr_ref, segc_ref, rows, index, low, blocks, block)
         outs, logs = [], []
         for h in range(heads):
             lanes = slice(h * width, (h + 1) * width)
@@ -342,19 +385,22 @@
             jax.ShapeDtypeStruct((length, width // 3), F32),
             jax.ShapeDtypeStruct((length, 8), F32),
         ),
-        in_specs=[pl.BlockSpec(memory_space=pltpu.SMEM)] + [VMEM_SPEC] * 4,
+        in_specs=[pl.BlockSpec(memory_space=pltpu.SMEM)] + [VMEM_SPEC] * 3,
         out_specs=(VMEM_SPEC,) * 3,
-    )(segments, qkv, segments, segments.reshape(length, 1), tiles)
+        scratch_shapes=[pltpu.VMEM((length, 8), F32)],
+        cost_estimate=pl.CostEstimate(flops=2 * length * length * width, bytes_accessed=8 << 20, transcendentals=heads * length * length),
+    )(segments, qkv, segments, tiles)
 
 
 def attend_back_kernel(
-    seg_smem, qkv_ref, segr_ref, segc_ref, tiles_ref, ctx32_ref, lse_ref, mixed_ref, wmix_ref, buckets_ref,
-    cots_ref, table_ref, do_ref, dk_ref, dv_ref, sums_ref,
+    seg_smem, qkv_ref, segr_ref, tiles_ref, ctx32_ref, lse_ref, mixed_ref, wmix_ref,
+    cots_ref, table_ref, segc_ref, do_ref, dk_ref, dv_ref, sums_ref,
 ):
     heads, kinds, block, _ = tiles_ref.shape
     length, width = qkv_ref.shape
     width = width // (3 * heads)
     count = length // block
+    segc_ref[...] = segment_column(segr_ref)
     dk_ref[...] = jnp.zeros_like(dk_ref)
     dv_ref[...] = jnp.zeros_like(dv_ref)
     sums_ref[...] = jnp.zeros_like(sums_ref)
@@ -367,14 +413,7 @@
 
     def run(index, low, blocks):
         rows = pl.ds(pl.multiple_of(index * block, block), block)
-        seg_q = segc_ref[rows, :]
-        places, sames, tile_at = [], [], []
-        for t in range(blocks):
-            j = low + t
-            place = pl.ds(pl.multiple_of(j * block, block), block)
-            places.append(place)
-            sames.append(seg_q == segr_ref[:, place])
-            tile_at.append(jnp.clip(j - index, -2, 2) + 2)
+        places, sames, tile_at = window_blocks(segr_ref, segc_ref, rows, index, low, blocks, block)
         product = do_ref[rows, :].astype(F32) * ctx32_ref[rows, :]
         logs = lse_ref[rows, :]
         outs = []
@@ -407,34 +446,42 @@
 
     both = [dk_ref[h] for h in range(heads)] + [dv_ref[h] for h in range(heads)]
     cots_ref[:, heads * width :] = jnp.concatenate(both, axis=1).astype(BF16)
-    lines = []
-    for h in range(heads):
-        for t in range(kinds):
-            if t in (0, kinds - 1):
+    near = [(h, t) for h in range(heads) for t in range(1, kinds - 1)]
+
+    def shifted(group, totals):
+        rows = pl.ds(pl.multiple_of(group * 8, 8), 8)
+        amount = lax.rem(2 * block - 8 * group, 2 * block)
+        out = []
+        for (h, t), total in zip(near, totals):
+            eight = sums_ref[h, t, rows, :]
+            wide = jnp.concatenate([eight, jnp.zeros_like(eight)], axis=1)
+            out.append(total + pltpu.roll(wide, amount, 1))
+        return tuple(out)
+
+    empty = jnp.zeros((8, 2 * block), F32)
+    totals = dict(zip(near, lax.fori_loop(0, block // 8, shifted, (empty,) * len(near))))
+    place = lax.broadcasted_iota(jnp.int32, empty.shape, 0)
+    result = jnp.zeros(table_ref.shape, F32)
+    for t in range(kinds):
+        lines = []
+        for h in range(heads):
+            if (h, t) in totals:
+                total = totals[h, t]
+                for bit in (1, 2, 4):
+                    total = jnp.where((place // bit) % 2 == 1, pltpu.roll(total, 2 * block - bit, 1), total)
+                lines.append(jnp.sum(total, axis=0, keepdims=True))
+            else:
                 line = jnp.sum(sums_ref[h, t], axis=0, keepdims=True)
                 lines.append(jnp.concatenate([line, jnp.zeros_like(line)], axis=1))
-                continue
-
-            def shifted(group, total):
-                eight = sums_ref[h, t, pl.ds(pl.multiple_of(group * 8, 8), 8), :]
-                wide = jnp.concatenate([eight, jnp.zeros_like(eight)], axis=1)
-                return total + pltpu.roll(wide, lax.rem(2 * block - 8 * group, 2 * block), 1)
-
-            total = lax.fori_loop(0, block // 8, shifted, jnp.zeros((8, 2 * block), F32))
-            place = lax.broadcasted_iota(jnp.int32, total.shape, 0)
-            for bit in (1, 2, 4):
-                total = jnp.where((place // bit) % 2 == 1, pltpu.roll(total, 2 * block - bit, 1), total)
-            lines.append(jnp.sum(total, axis=0, keepdims=True))
-    total = jnp.zeros(table_ref.shape, F32)
-    for t in range(kinds):
-        line = jnp.concatenate([lines[h * kinds + t] for h in range(heads)] + [jnp.zeros((8 - heads, 2 * block), F32)], axis=0)
-        total += lax.dot_general(
-            line, buckets_ref[t], (((1,), (0,)), ((), ())), precision=lax.Precision.HIGHEST, preferred_element_type=F32
+        lines.append(jnp.zeros((8 - heads, 2 * block), F32))
+        result += lax.dot_general(
+            jnp.concatenate(lines, axis=0), bucket_onehot(t, block, 128),
+            (((1,), (1,)), ((), ())), precision=HIGHEST, preferred_element_type=F32,
         )
-    table_ref[...] = total
-
-
-def attend_back(qkv, segments, tiles, ctx32, lse, mixed, wmix, buckets):
+    table_ref[...] = result
+
+
+def attend_back(qkv, segments, tiles, ctx32, lse, mixed, wmix):
     length, width = qkv.shape
     heads, _, block, _ = tiles.shape
     size = width // (3 * heads)
@@ -445,18 +492,20 @@
             jax.ShapeDtypeStruct((length, width), BF16),
             jax.ShapeDtypeStruct((8, 128), F32),
         ),
-        in_specs=[pl.BlockSpec(memory_space=pltpu.SMEM)] + [VMEM_SPEC] * 9,
+        in_specs=[pl.BlockSpec(memory_space=pltpu.SMEM)] + [VMEM_SPEC] * 7,
         out_specs=(VMEM_SPEC,) * 2,
+        cost_estimate=pl.CostEstimate(flops=8 * length * length * width, bytes_accessed=32 << 20, transcendentals=heads * length * length),
         scratch_shapes=[
+            pltpu.VMEM((length, 8), F32),
             pltpu.VMEM((length, width // 3), BF16),
             pltpu.VMEM((heads, length, size), F32),
             pltpu.VMEM((heads, length, size), F32),
             pltpu.VMEM((heads, 5, block, block), F32),
         ],
-    )(segments, qkv, segments, segments.reshape(length, 1), tiles, ctx32, lse, mixed, wmix, buckets)
-
-
-def block_rows(place, owner, size):
+    )(segments, qkv, segments, tiles, ctx32, lse, mixed, wmix)
+
+
+def block_rows(owner, size):
     return pl.ds(pl.multiple_of(owner * size, size), size)
 
 
@@ -469,36 +518,73 @@
     return inside, row - 8 * (row // 8)
 
 
+def gain_spread(n, features):
+    count = features // (4 * n)
+    lane = lax.broadcasted_iota(jnp.int32, (128, features), 1)
+    row = lax.broadcasted_iota(jnp.int32, (128, features), 0)
+    share = ((lane.astype(F32) + 0.5) * (1.0 / count)).astype(jnp.int32)
+    return (lane - share * count == row).astype(F32)
+
+
+def widened(part, width):
+    spare = width - part.shape[1]
+    part = part.astype(BF16)
+    if spare:
+        part = jnp.concatenate([part, jnp.zeros((part.shape[0], spare), BF16)], axis=1)
+    return part
+
+
+def flat(ref):
+    return ref[...].reshape(-1, ref.shape[2])
+
+
+def transpose_slots(source, target):
+    n, width, _ = target.shape
+    for pair in range(n // 2):
+        both = source[:, 2 * width * pair : 2 * width * (pair + 1)].T
+        target[2 * pair] = both[:width]
+        target[2 * pair + 1] = both[width:]
+
+
 def enter_kernel(
-    n, x_ref, cot_ref, gain_ref, spread_ref, w_ref, wgate_ref, line_ref,
-    normed_out, cot_out, wgate_out, qkv_ref, wqkv_ref, wmix_ref, gains_ref, tiles_ref,
-    wfull, gfull, nfull, cfull, g4, g32,
+    n, x_ref, cot_ref, gain_ref, gain_two_ref, wq_ref, wk_ref, wv_ref, wm_ref, wg_ref, wl_ref, wd_ref, table_ref,
+    normed_out, cot_out, wgate_out, qkv_out, wqkv_out, wmix_out, tiles_out, lift_ref, down_ref, gains_ref,
+    wfull, gfull, nfull, cfull, normed_t, cot_t, g1, g4, g32, qkv_v, wqkv_v, wmix_v, tiles_v,
     ring_send, ring_recv, gate_send, gate_recv, pair_send, pair_recv, cot_send, cot_recv,
-    g_send, g_recv, h_send, h_recv, local_sem,
+    g_send, g_recv, h_send, h_recv, local_sem, out_sem,
 ):
     place = Place(n)
-    size = x_ref.shape[0]
-    own_w = pltpu.make_async_copy(w_ref, wfull.at[place.d], local_sem.at[0])
-    own_g = pltpu.make_async_copy(gain_ref, g4.at[place.m], local_sem.at[1])
-    own_gate = pltpu.make_async_copy(wgate_ref, gfull.at[place.d], local_sem.at[2])
-    for copy in (own_w, own_g, own_gate):
-        copy.start()
+    size, features = x_ref.shape
+    per = gain_ref.shape[0]
+    wide = gfull.shape[2]
+    heads = wq_ref.shape[1]
+    g1[...] = jnp.zeros_like(g1)
+    g1[0:1, 0:per] = gain_ref[...].reshape(1, per)
+    g1[1:2, 0:per] = gain_two_ref[...].reshape(1, per)
+    for k, ref in enumerate((wq_ref, wk_ref, wv_ref)):
+        wfull[place.d, :, k * heads : (k + 1) * heads] = ref[...].astype(BF16)
+    wfull[place.d, :, 3 * heads :] = wm_ref[...].T.astype(BF16)
+    gfull[place.d] = widened(wg_ref[...], wide)
+    own_g = pltpu.make_async_copy(g1, g4.at[place.m], local_sem.at[0])
+    own_g.start()
     place.barrier(everyone=True)
     ring = RingGather(place, wfull, ring_send, ring_recv)
     gate_ring = RingGather(place, gfull, gate_send, gate_recv)
     small = [
-        remote(gain_ref, g4.at[place.m], g_send.at[k], g_recv.at[k], {"mp": lax.rem(place.m + k, 4)})
+        remote(g1, g4.at[place.m], g_send.at[k], g_recv.at[k], {"mp": lax.rem(place.m + k, 4)})
         for k in range(1, 4)
     ]
     for copy in small:
         copy.start()
-    own_w.wait()
-    own_gate.wait()
-    for way in (0, 1):
-        ring.advance(way, 0)
+
+    def both(which, step):
+        for way in (0, 1):
+            which.advance(way, step)
+
+    both(ring, 0)
+    both(gate_ring, 0)
     scale = norm_scale(x_ref[...])
-    rows = block_rows(place, place.m, size)
-    cfull[rows, :] = cot_ref[...].astype(BF16)
+    rows = block_rows(place.m, size)
     own_g.wait()
     for k in range(1, 4):
         slot = g4.at[lax.rem(place.m + 4 - k, 4)]
@@ -509,20 +595,19 @@
     ]
     for copy in around:
         copy.start()
-    own_h = pltpu.make_async_copy(g4, g32.at[place.d], local_sem.at[1])
+    own_h = pltpu.make_async_copy(g4, g32.at[place.d], local_sem.at[0])
     own_h.start()
-    for way in (0, 1):
-        gate_ring.advance(way, 0)
+    cfull[rows, :] = cot_ref[...].astype(BF16)
+    spread = gain_spread(n, features).astype(BF16)
     own_h.wait()
     for k in range(1, n):
         slot = g32.at[lax.rem(place.d + n - k, n)]
         remote(g4, slot, h_send.at[k], h_recv.at[k], {"dp": place.right}).wait_recv()
     pieces = g32[...].reshape(-1, 128).astype(BF16)
-    wide = matmul(pieces, spread_ref[...])
-    inside, kind = gain_lanes(n, wide.shape)
-    gain = jnp.sum(jnp.where(inside & (kind == 0), wide, 0.0), axis=0, keepdims=True)
-    gain_two = jnp.sum(jnp.where(inside & (kind == 1), wide, 0.0), axis=0, keepdims=True)
-    gains_ref[...] = jnp.concatenate([gain, gain_two] + [jnp.zeros_like(gain)] * 6, axis=0)
+    spaced = matmul(pieces, spread)
+    inside, kind = gain_lanes(n, spaced.shape)
+    gain = jnp.sum(jnp.where(inside & (kind == 0), spaced, 0.0), axis=0, keepdims=True)
+    gain_two = jnp.sum(jnp.where(inside & (kind == 1), spaced, 0.0), axis=0, keepdims=True)
     nfull[rows, :] = (x_ref[...] * scale * gain).astype(BF16)
     pair = PairGather(place, nfull, pair_send, pair_recv)
     cots = PairGather(place, cfull, cot_send, cot_recv)
@@ -530,135 +615,155 @@
         pair.begin(chunk)
     for chunk in range(2):
         cots.begin(chunk)
-    bias_tiles(line_ref, tiles_ref)
-    for step in (1, 2):
-        for way in (0, 1):
-            ring.advance(way, step)
-        if step == 1:
-            pair.relay(0)
-        for way in (0, 1):
-            gate_ring.advance(way, step)
+    gains_ref[...] = jnp.concatenate([gain, gain_two] + [jnp.zeros_like(gain)] * 6, axis=0)
+    both(ring, 1)
+    lift_ref[...] = widened(wl_ref[...], wide)
+    down_ref[...] = widened(wd_ref[...], wide)
+    both(gate_ring, 1)
+    pair.relay(0)
+    bias_tiles(table_ref, tiles_v)
+    out_t = pltpu.make_async_copy(tiles_v, tiles_out, out_sem.at[0])
+    out_t.start()
+    both(ring, 2)
     pair.relay(1)
-    for way in (0, 1):
-        ring.advance(way, 3)
+    both(gate_ring, 2)
     for chunk in range(2):
         pair.end(chunk)
-    out_n = pltpu.make_async_copy(nfull, normed_out, local_sem.at[2])
+    transpose_slots(nfull, normed_t)
+    out_n = pltpu.make_async_copy(normed_t, normed_out, out_sem.at[1])
     out_n.start()
+    both(ring, 3)
+    both(gate_ring, 3)
+    cots.relay(0)
     for step in range(4, n // 2 + 1):
-        for way in (0, 1):
-            ring.advance(way, step)
-    for way in (0, 1):
-        gate_ring.advance(way, 3)
-    cots.relay(0)
-    width = qkv_ref.shape[1]
-    wqkv_ref[...] = wfull[:, :, :width]
-    wmix_ref[...] = wfull[:, :, width:]
-    weight = wqkv_ref[...].reshape(-1, width)
+        both(ring, step)
+    wqkv_v[...] = wfull[:, :, : 3 * heads]
+    wmix_v[...] = wfull[:, :, 3 * heads :]
+    out_w = pltpu.make_async_copy(wqkv_v, wqkv_out, out_sem.at[2])
+    out_m = pltpu.make_async_copy(wmix_v, wmix_out, out_sem.at[3])
+    out_w.start()
+    out_m.start()
 
     @pl.loop(0, 4)
     def _(block):
-        rows = pl.ds(pl.multiple_of(block * size, size), size)
-        qkv_ref[rows, :] = matmul(nfull[rows, :], weight).astype(BF16)
-
+        rows = block_rows(block, size)
+        qkv_v[rows, :] = matmul(nfull[rows, :], flat(wqkv_v)).astype(BF16)
+
+    out_q = pltpu.make_async_copy(qkv_v, qkv_out, out_sem.at[4])
+    out_q.start()
     cots.relay(1)
-    for step in range(4, n // 2 + 1):
-        for way in (0, 1):
-            gate_ring.advance(way, step)
-    out_g = pltpu.make_async_copy(gfull, wgate_out, local_sem.at[0])
-    out_g.start()
     for chunk in range(2):
         cots.end(chunk)
-    out_c = pltpu.make_async_copy(cfull, cot_out, local_sem.at[1])
+    transpose_slots(cfull, cot_t)
+    out_c = pltpu.make_async_copy(cot_t, cot_out, out_sem.at[6])
     out_c.start()
+    for step in range(4, n // 2 + 1):
+        both(gate_ring, step)
+    out_g = pltpu.make_async_copy(gfull, wgate_out, out_sem.at[5])
+    out_g.start()
     ring.finish()
     gate_ring.finish()
+    pair.finish()
+    cots.finish()
     for copy in small + around:
         copy.wait_send()
-    out_n.wait()
-    out_g.wait()
-    out_c.wait()
-
-
-def enter(n, x, cot, gain, spread, weights, wgate, lines, kinds=5):
+    for copy in (out_t, out_n, out_w, out_m, out_q, out_g, out_c):
+        copy.wait()
+
+
+def enter(n, x, cot, gain, gain_two, wq, wk, wv, wm, wg, wl, wd, table):
     size, features = x.shape
-    rows, columns = weights.shape
-    wide = wgate.shape[1]
-    heads = columns // 4
-    count = (lines.shape[0] - 1) // kinds
-    block = lines.shape[1] // 2
+    rows, heads = wq.shape
+    wide = wg.shape[1] + -wg.shape[1] % 128
+    count = table.shape[0]
+    shape = jax.ShapeDtypeStruct
+    outs = (
+        shape((n, features // n, 4 * size), BF16),
+        shape((n, features // n, 4 * size), BF16),
+        shape((n, rows, wide), BF16),
+        shape((4 * size, 3 * heads), BF16),
+        shape((n, rows, 3 * heads), BF16),
+        shape((n, rows, heads), BF16),
+        shape((count, KINDS, BLOCK, BLOCK), F32),
+        shape((rows, wide), BF16),
+        shape((rows, wide), BF16),
+        shape((8, features), F32),
+    )
     return pl.pallas_call(
         functools.partial(enter_kernel, n),
         name="enter",
-        out_shape=(
-            jax.ShapeDtypeStruct((4 * size, features), BF16),
-            jax.ShapeDtypeStruct((4 * size, features), BF16),
-            jax.ShapeDtypeStruct((n, rows, wide), BF16),
-            jax.ShapeDtypeStruct((4 * size, 3 * heads), BF16),
-            jax.ShapeDtypeStruct((n, rows, 3 * heads), BF16),
-            jax.ShapeDtypeStruct((n, rows, heads), BF16),
-            jax.ShapeDtypeStruct((8, features), F32),
-            jax.ShapeDtypeStruct((count, kinds, block, block), F32),
-        ),
-        in_specs=[VMEM_SPEC] * 7,
-        out_specs=(ANY_SPEC,) * 3 + (VMEM_SPEC,) * 5,
+        out_shape=outs,
+        in_specs=[VMEM_SPEC] * 12,
+        out_specs=(ANY_SPEC,) * 7 + (VMEM_SPEC,) * 3,
         scratch_shapes=[
-            pltpu.VMEM((n, rows, columns), BF16),
+            pltpu.VMEM((n, rows, 4 * heads), BF16),
             pltpu.VMEM((n, rows, wide), BF16),
             pltpu.VMEM((4 * size, features), BF16),
             pltpu.VMEM((4 * size, features), BF16),
+            pltpu.VMEM(outs[0].shape, BF16),
+            pltpu.VMEM(outs[1].shape, BF16),
+            pltpu.VMEM((8, 128), F32),
             pltpu.VMEM((4, 8, 128), F32),
             pltpu.VMEM((n, 4, 8, 128), F32),
+            *(pltpu.VMEM(outs[k].shape, outs[k].dtype) for k in (3, 4, 5, 6)),
             DMA((2, n // 2)), DMA((2, n // 2)),
             DMA((2, n // 2)), DMA((2, n // 2)),
             DMA((3, 2)), DMA((3, 2)),
             DMA((3, 2)), DMA((3, 2)),
             DMA((4,)), DMA((4,)),
             DMA((n,)), DMA((n,)),
-            DMA((3,)),
+            DMA((1,)), DMA((7,)),
         ],
         compiler_params=pltpu.CompilerParams(collective_id=0, has_side_effects=True),
-    )(x, cot, gain, spread, weights, wgate, lines)
+    )(x, cot, gain, gain_two, wq, wk, wv, wm, wg, wl, wd, table)
 
 
 def middle_kernel(
-    n, ctx_ref, wmix_ref, x_ref, gains_ref, wlift_ref, wdown_ref, wgate_any,
+    n, ctx_ref, wmix_ref, x_ref, gains_ref, lift_ref, from_left_ref, from_right_ref, down_ref, wgate_any,
     second_out, lift_out, down_out, bend_out, slope_out, hidden_out, middle_ref,
-    lfull, dfull, gate_v, sfull, own_v, bend_v, slope_v, hidden_v,
+    lfull, dfull, gate_v, sfull, second_t, own_v, bend_v, slope_v, hidden_v,
     give, got, over, came, sc_send, sc_recv,
     pair_send, pair_recv, lift_send, lift_recv, down_send, down_recv, local_sem, out_sem,
 ):
     place = Place(n)
     size = x_ref.shape[0]
-    own_l = pltpu.make_async_copy(wlift_ref, lfull.at[place.d], local_sem.at[0])
-    own_d = pltpu.make_async_copy(wdown_ref, dfull.at[place.d], local_sem.at[1])
-    load_g = pltpu.make_async_copy(wgate_any, gate_v, local_sem.at[2])
-    for copy in (own_l, own_d, load_g):
+    starts = [
+        pltpu.make_async_copy(source, target, local_sem.at[k])
+        for k, (source, target) in enumerate(
+            (
+                (from_left_ref, lfull.at[place.left]),
+                (from_right_ref, lfull.at[place.right]),
+                (lift_ref, lfull.at[place.d]),
+                (down_ref, dfull.at[place.d]),
+                (wgate_any, gate_v),
+            )
+        )
+    ]
+    for copy in starts:
         copy.start()
     place.barrier()
-    lift = RingGather(place, lfull, lift_send, lift_recv)
+    lift = RingGather(place, lfull, lift_send, lift_recv, first=1)
     down = RingGather(place, dfull, down_send, down_recv)
     scatter = PairScatter(place, give, got, over, came, sc_send, sc_recv)
     pair = PairGather(place, sfull, pair_send, pair_recv)
-    own_l.wait()
-    own_d.wait()
 
     def both(ring, step):
         for way in (0, 1):
             ring.advance(way, step)
 
-    both(lift, 0)
-    weight = wmix_ref[...].reshape(-1, wmix_ref.shape[2])
+    for copy in starts[:4]:
+        copy.wait()
+    both(lift, 1)
+    both(down, 0)
 
     def part(owner):
-        return matmul_nt(ctx_ref[block_rows(place, owner, size), :], weight)
+        return matmul_nt(ctx_ref[block_rows(owner, size), :], flat(wmix_ref))
 
     scatter.far(part(place.far))
     scatter.twin(part(place.twin))
     scatter.mate(part(place.mate))
     own_v[...] = part(place.m)
-    both(down, 0)
-    both(lift, 1)
+    both(lift, 2)
     gain = gains_ref[1:2, :]
     chunk_rows = size // 2
     for chunk in range(2):
@@ -668,83 +773,88 @@
         start = pl.multiple_of(place.m * size + chunk * chunk_rows, chunk_rows)
         sfull[pl.ds(start, chunk_rows), :] = (middle * norm_scale(middle) * gain).astype(BF16)
         pair.begin(chunk)
-    load_g.wait()
-
-    def gate_block(owner):
-        rows = block_rows(place, owner, size)
-        gate = matmul(sfull[rows, :], gate_v[...].reshape(-1, gate_v.shape[2]))
-        bend, slope = gate_terms(gate)
+    both(down, 1)
+    starts[4].wait()
+
+    def gate_block(k, _=None):
+        rows = block_rows(lax.rem(place.m + k, 4), size)
+        bend, slope = gate_terms(matmul(sfull[rows, :], flat(gate_v)))
         bend_v[rows, :] = bend
         slope_v[rows, :] = slope
 
-    gate_block(place.m)
-    both(down, 1)
-    both(lift, 2)
-    pair.relay(0)
-    pair.relay(1)
-    both(down, 2)
-    both(lift, 3)
-    for chunk in range(2):
-        pair.end(chunk)
-    out_s = pltpu.make_async_copy(sfull, second_out, local_sem.at[0])
+    @pl.loop(0, 4)
+    def _(k):
+        @pl.when(k == 1)
+        def _():
+            both(lift, 3)
+            pair.relay(0)
+            both(down, 2)
+            pair.relay(1)
+            for chunk in range(2):
+                pair.end(chunk)
+
+        gate_block(k)
+
+    transpose_slots(sfull, second_t)
+    out_s = pltpu.make_async_copy(second_t, second_out, out_sem.at[0])
+    out_b = pltpu.make_async_copy(bend_v, bend_out, out_sem.at[1])
     out_s.start()
-
-    @pl.loop(1, 4)
-    def _(k):
-        gate_block(lax.rem(place.m + k, 4))
-
-    both(lift, 4)
-    out_b = pltpu.make_async_copy(bend_v, bend_out, local_sem.at[1])
     out_b.start()
-    out_l = pltpu.make_async_copy(lfull, lift_out, local_sem.at[2])
+    for step in range(4, n // 2 + 1):
+        both(lift, step)
+    out_l = pltpu.make_async_copy(lfull, lift_out, out_sem.at[2])
     out_l.start()
     both(down, 3)
 
     @pl.loop(0, 4)
     def _(k):
-        rows = pl.ds(pl.multiple_of(k * size, size), size)
-        lifted = matmul(sfull[rows, :], lfull[...].reshape(-1, lfull.shape[2]))
+        rows = block_rows(k, size)
+        lifted = matmul(sfull[rows, :], flat(lfull))
         hidden_v[rows, :] = (bend_v[rows, :] * lifted).astype(BF16)
         slope_v[rows, :] = slope_v[rows, :] * lifted
 
-    out_p = pltpu.make_async_copy(slope_v, slope_out, out_sem.at[0])
-    out_h = pltpu.make_async_copy(hidden_v, hidden_out, out_sem.at[1])
-    out_d = pltpu.make_async_copy(dfull, down_out, out_sem.at[2])
+    out_p = pltpu.make_async_copy(slope_v, slope_out, out_sem.at[3])
+    out_h = pltpu.make_async_copy(hidden_v, hidden_out, out_sem.at[4])
+    out_d = pltpu.make_async_copy(dfull, down_out, out_sem.at[5])
     out_p.start()
     out_h.start()
-    both(down, 4)
+    for step in range(4, n // 2 + 1):
+        both(down, step)
     out_d.start()
     lift.finish()
     down.finish()
     scatter.finish()
+    pair.finish()
     for copy in (out_s, out_b, out_l, out_p, out_h, out_d):
         copy.wait()
 
 
-def middle_part(n, ctx, wmix, x, gains, wlift, wdown, wgate):
+def middle_part(n, ctx, wmix, x, gains, lift, from_left, from_right, down, wgate):
     size, features = x.shape
-    rows, wide = wlift.shape
+    rows, wide = lift.shape
     length = 4 * size
-    full = jax.ShapeDtypeStruct((n, rows, wide), BF16)
+    shape = jax.ShapeDtypeStruct
+    full = shape((n, rows, wide), BF16)
     return pl.pallas_call(
         functools.partial(middle_kernel, n),
         name="middle",
         out_shape=(
-            jax.ShapeDtypeStruct((length, features), BF16),
+            shape((n, features // n, length), BF16),
             full,
             full,
-            jax.ShapeDtypeStruct((length, wide), F32),
-            jax.ShapeDtypeStruct((length, wide), F32),
-            jax.ShapeDtypeStruct((length, wide), BF16),
-            jax.ShapeDtypeStruct((size, features), F32),
+            shape((length, wide), F32),
+            shape((length, wide), F32),
+            shape((length, wide), BF16),
+            shape((size, features), F32),
         ),
-        in_specs=[VMEM_SPEC] * 6 + [ANY_SPEC],
+        in_specs=[VMEM_SPEC] * 8 + [ANY_SPEC],
         out_specs=(ANY_SPEC,) * 6 + (VMEM_SPEC,),
         scratch_shapes=[
             pltpu.VMEM((n, rows, wide), BF16),
             pltpu.VMEM((n, rows, wide), BF16),
             pltpu.VMEM((n, rows, wide), BF16),
             pltpu.VMEM((length, features), BF16),
+            pltpu.VMEM((n, features // n, length), BF16),
             pltpu.VMEM((size, features), F32),
             pltpu.VMEM((length, wide), F32),
             pltpu.VMEM((length, wide), F32),
@@ -753,10 +863,10 @@
             DMA((3, 2)), DMA((3, 2)),
             DMA((2, n // 2)), DMA((2, n // 2)),
             DMA((2, n // 2)), DMA((2, n // 2)),
-            DMA((3,)), DMA((3,)),
+            DMA((5,)), DMA((6,)),
         ],
         compiler_params=pltpu.CompilerParams(collective_id=1, has_side_effects=True),
-    )(ctx, wmix, x, gains, wlift, wdown, wgate)
+    )(ctx, wmix, x, gains, lift, from_left, from_right, down, wgate)
 
 
 def norm_back(values, gain, grad):
@@ -767,135 +877,190 @@
 
 
 def back_kernel(
-    n, middle_ref, cotangent_ref, gains_ref, hidden_any, cot_any, second_any, bend_any, slope_any, wgate_any, wlift_any, wdown_any,
-    mixed_out, middle_cot_ref, feed_ref, grad_down_ref, grad_gate_ref, grad_lift_ref,
-    hidden_v, cot_v, second_v, gate_v, lift_v, down_v, bend_v, slope_v, gcot_v, lcot_v, mixed_v, own_v,
+    n, middle_ref, gains_ref, cotangent_any, hidden_any, cot_any, second_any, bend_any, slope_any, wgate_any, wlift_any, wdown_any,
+    mixed_out, pending_out, output_out, middle_cot_out, feed_ref, own_ref,
+    hidden_v, cot_v, gate_v, lift_v, down_v, bend_v, slope_v, gcot_v, lcot_v, mixed_v, part_v, part_two_v,
     give, got, over, came, sc_send, sc_recv,
+    give_two, got_two, over_two, came_two, sd_send, sd_recv,
     pair_send, pair_recv,
-    put_d, in_d, send_d, recv_d, put_g, in_g, send_g, recv_g, put_l, in_l, send_l, recv_l,
-    load_sem, piece_sem, out_sem,
+    put_g, in_g, send_g, recv_g, put_l, in_l, send_l, recv_l, put_d, in_d, send_d, recv_d,
+    load_sem, piece_sem, pend_sem, out_sem,
 ):
     place = Place(n)
     size = middle_ref.shape[0]
     loads = [
         pltpu.make_async_copy(source, target, load_sem.at[k])
         for k, (source, target) in enumerate(
-            ((hidden_any, hidden_v), (cot_any, cot_v), (wdown_any, down_v), (wgate_any, gate_v), (wlift_any, lift_v), (second_any, second_v))
+            ((hidden_any, hidden_v), (cot_any, cot_v), (wdown_any, down_v), (wgate_any, gate_v), (wlift_any, lift_v), (cotangent_any, part_two_v))
         )
     ]
     for copy in loads:
         copy.start()
-    order = (place.far, place.twin, place.mate, place.m)
+
+    def owner_of(k):
+        core = lax.rem(place.m + 3 - k, 2)
+        chip = lax.rem(place.m // 2 + (3 - k) // 2, 2)
+        return 2 * chip + core
 
     def pieces(k):
-        rows = block_rows(place, order[k], size)
+        rows = block_rows(owner_of(k), size)
         return [
-            pltpu.make_async_copy(source.at[rows], target.at[k % 2], piece_sem.at[k % 2, i])
+            pltpu.make_async_copy(source.at[rows], target.at[lax.rem(k, 2)], piece_sem.at[lax.rem(k, 2), i])
             for i, (source, target) in enumerate(((bend_any, bend_v), (slope_any, slope_v)))
         ]
 
     for copy in pieces(0):
         copy.start()
     place.barrier()
-    down = RingScatter(place, lambda slot: matmul_tn(slot_columns(cot_v, slot, n), hidden_v[...]), grad_down_ref, put_d, in_d, send_d, recv_d)
-    gate = RingScatter(place, lambda slot: matmul_tn(slot_columns(second_v, slot, n), gcot_v[...]), grad_gate_ref, put_g, in_g, send_g, recv_g)
-    lift = RingScatter(place, lambda slot: matmul_tn(slot_columns(second_v, slot, n), lcot_v[...]), grad_lift_ref, put_l, in_l, send_l, recv_l)
+    gate = RingScatter(place, lambda slot: matmul(gate_v[slot], gcot_v[...]), put_g, in_g, send_g, recv_g, 0)
+    lift = RingScatter(place, lambda slot: matmul(gate_v[slot], lcot_v[...]), put_l, in_l, send_l, recv_l, 1)
+    down = RingScatter(place, lambda slot: matmul(cot_v[slot], hidden_v[...]), put_d, in_d, send_d, recv_d, 2)
     scatter = PairScatter(place, give, got, over, came, sc_send, sc_recv)
+    downs = PairScatter(place, give_two, got_two, over_two, came_two, sd_send, sd_recv)
     pair = PairGather(place, mixed_v, pair_send, pair_recv)
 
-    def both(ring, step):
-        for way in (0, 1):
-            ring.advance(way, step)
-
-    def flat(ref):
-        return ref[...].reshape(-1, ref.shape[2])
+    def hand(ring):
+        return [
+            pltpu.make_async_copy(ring.put.at[way, 0], pending_out.at[way, ring.last], pend_sem.at[ring.last, way])
+            for way in (0, 1)
+        ]
 
     loads[0].wait()
     loads[1].wait()
-    both(down, 0)
+    down.advance(0)
     for copy in loads[2:5]:
         copy.wait()
-    for k in range(4):
-        rows = block_rows(place, order[k], size)
-        if k < 3:
+
+    @pl.loop(0, 4)
+    def _(k):
+        rows = block_rows(owner_of(k), size)
+
+        @pl.when(k < 3)
+        def _():
             for copy in pieces(k + 1):
                 copy.start()
-        hidden_cot = matmul(cot_v[rows, :], flat(down_v))
+
+        hidden_cot = matmul_tn(cot_v[:, :, rows].reshape(-1, size), flat(down_v))
         for copy in pieces(k):
             copy.wait()
-        gate_cot = (hidden_cot * slope_v[k % 2]).astype(BF16)
-        lift_cot = (hidden_cot * bend_v[k % 2]).astype(BF16)
-        gcot_v[rows, :] = gate_cot
-        lcot_v[rows, :] = lift_cot
-        part = matmul_nt(gate_cot, flat(gate_v)) + matmul_nt(lift_cot, flat(lift_v))
-        if k == 0:
-            scatter.far(part)
-        elif k == 1:
-            scatter.twin(part)
-            both(down, 1)
-        elif k == 2:
-            scatter.mate(part)
-        else:
-            own_v[...] = part
+        gcot_v[rows, :] = (hidden_cot * slope_v[lax.rem(k, 2)]).astype(BF16)
+        lcot_v[rows, :] = (hidden_cot * bend_v[lax.rem(k, 2)]).astype(BF16)
+        part_v[...] = matmul_nt(gcot_v[rows, :], flat(gate_v)) + matmul_nt(lcot_v[rows, :], flat(lift_v))
+
+        @pl.when(k == 0)
+        def _():
+            scatter.far(part_v[...])
+
+        @pl.when(k == 1)
+        def _():
+            scatter.twin(part_v[...])
+            down.advance(1)
+
+        @pl.when(k == 2)
+        def _():
+            scatter.mate(part_v[...])
+
+    load_second = pltpu.make_async_copy(second_any, gate_v, load_sem.at[3])
+    load_second.start()
+    down.advance(2)
+    load_second.wait()
+    gate.advance(0)
+    lift.advance(0)
     loads[5].wait()
-    both(gate, 0)
-    both(down, 2)
-    both(lift, 0)
     chunk_rows = size // 2
     gain = gains_ref[1:2, :]
     feed = jnp.zeros_like(gain)
     for chunk in range(2):
         rows = slice(chunk * chunk_rows, (chunk + 1) * chunk_rows)
-        grad = scatter.take(chunk, own_v[rows, :])
+        grad = scatter.take(chunk, part_v[rows, :])
         through, term = norm_back(middle_ref[rows, :], gain, grad)
-        middle_cot = cotangent_ref[rows, :] + through
-        middle_cot_ref[rows, :] = middle_cot
+        middle_cot = part_two_v[rows, :] + through
+        part_v[rows, :] = middle_cot
         feed += jnp.sum(term, axis=0, keepdims=True)
         start = pl.multiple_of(place.m * size + chunk * chunk_rows, chunk_rows)
         mixed_v[pl.ds(start, chunk_rows), :] = middle_cot.astype(BF16)
         pair.begin(chunk)
+    out_c = pltpu.make_async_copy(part_v, middle_cot_out, out_sem.at[0])
+    out_c.start()
     feed_ref[...] = jnp.concatenate([feed] + [jnp.zeros_like(feed)] * 7, axis=0)
-    scatter.finish()
-    both(gate, 1)
-    both(down, 3)
-    both(lift, 1)
+    gate.advance(1)
+    down.advance(3)
+    for copy in hand(down):
+        copy.start()
+    lift.advance(1)
+
+    @pl.loop(0, 4)
+    def _(k):
+        part_two_v[...] = matmul_nt(hidden_v[block_rows(owner_of(k), size), :], flat(down_v))
+
+        @pl.when(k == 0)
+        def _():
+            downs.far(part_two_v[...])
+
+        @pl.when(k == 1)
+        def _():
+            downs.twin(part_two_v[...])
+
+        @pl.when(k == 2)
+        def _():
+            downs.mate(part_two_v[...])
+
     pair.relay(0)
     pair.relay(1)
-    both(gate, 2)
-    down.finish()
-    both(lift, 2)
+    gate.advance(2)
+    own_ref[2] = down.total()
+    lift.advance(2)
     for chunk in range(2):
         pair.end(chunk)
-    out_m = pltpu.make_async_copy(mixed_v, mixed_out, out_sem.at[0])
+    out_m = pltpu.make_async_copy(mixed_v, mixed_out, out_sem.at[1])
     out_m.start()
-    both(gate, 3)
-    both(lift, 3)
-    gate.finish()
-    lift.finish()
+    own_ref[0] = gate.total()
+    own_ref[1] = lift.total()
+    for chunk in range(2):
+        rows = slice(chunk * chunk_rows, (chunk + 1) * chunk_rows)
+        part_two_v[rows, :] = middle_ref[rows, :] + downs.take(chunk, part_two_v[rows, :])
+    out_o = pltpu.make_async_copy(part_two_v, output_out, out_sem.at[2])
+    out_o.start()
+    gate.advance(3)
+    for copy in hand(gate):
+        copy.start()
+    lift.advance(3)
+    for copy in hand(lift):
+        copy.start()
+    for ring in (gate, lift, down):
+        ring.finish()
+        for copy in hand(ring):
+            copy.wait()
+    scatter.finish()
+    downs.finish()
+    pair.finish()
+    out_c.wait()
     out_m.wait()
+    out_o.wait()
 
 
 def back_part(n, middle, cotangent, gains, hidden, cot, second, bend, slope, wgate, wlift, wdown):
     size, features = middle.shape
     length, wide = hidden.shape
     rows = wgate.shape[1]
-    grad = jax.ShapeDtypeStruct((rows, wide), F32)
+    shape = jax.ShapeDtypeStruct
     weight = pltpu.VMEM((n, rows, wide), BF16)
     return pl.pallas_call(
         functools.partial(back_kernel, n),
         name="back",
         out_shape=(
-            jax.ShapeDtypeStruct((length, features), BF16),
-            jax.ShapeDtypeStruct((size, features), F32),
-            jax.ShapeDtypeStruct((8, features), F32),
-            grad, grad, grad,
+            shape((length, features), BF16),
+            shape((2, 3, rows, wide), BF16),
+            shape((size, features), F32),
+            shape((size, features), F32),
+            shape((8, features), F32),
+            shape((3, rows, wide), F32),
         ),
-        in_specs=[VMEM_SPEC] * 3 + [ANY_SPEC] * 8,
-        out_specs=(ANY_SPEC,) + (VMEM_SPEC,) * 5,
+        in_specs=[VMEM_SPEC] * 2 + [ANY_SPEC] * 9,
+        out_specs=(ANY_SPEC,) * 4 + (VMEM_SPEC,) * 2,
         scratch_shapes=[
             pltpu.VMEM((length, wide), BF16),
-            pltpu.VMEM((length, features), BF16),
-            pltpu.VMEM((length, features), BF16),
+            pltpu.VMEM((n, features // n, length), BF16),
             weight, weight, weight,
             pltpu.VMEM((2, size, wide), F32),
             pltpu.VMEM((2, size, wide), F32),
@@ -903,35 +1068,34 @@
             pltpu.VMEM((length, wide), BF16),
             pltpu.VMEM((length, features), BF16),
             pltpu.VMEM((size, features), F32),
+            pltpu.VMEM((size, features), F32),
+            *PairScatter.scratch(size, features),
             *PairScatter.scratch(size, features),
             DMA((3, 2)), DMA((3, 2)),
-            *RingScatter.scratch(n, rows, wide),
-            *RingScatter.scratch(n, rows, wide),
-            *RingScatter.scratch(n, rows, wide),
-            DMA((6,)), DMA((2, 2)), DMA((1,)),
+            *RingScatter.scratch(n, rows, wide, 1),
+            *RingScatter.scratch(n, rows, wide, 1),
+            *RingScatter.scratch(n, rows, wide, 1),
+            DMA((6,)), DMA((2, 2)), DMA((3, 2)), DMA((3,)),
         ],
         compiler_params=pltpu.CompilerParams(collective_id=2, has_side_effects=True, vmem_limit_bytes=67043328),
-    )(middle, cotangent, gains, hidden, cot, second, bend, slope, wgate, wlift, wdown)
+    )(middle, gains, cotangent, hidden, cot, second, bend, slope, wgate, wlift, wdown)
 
 
 def leave_kernel(
-    n, cots_ref, ctx_ref, wqkv_ref, x_ref, gains_ref, middle_cot_ref, feed_ref, table_ref, spread_ref,
-    middle_ref, hidden_ref, normed_any, mixed_any, wdown_any,
-    grad_ref, gain_out, table_out, input_ref, output_ref,
-    normed_v, mixed_v, down_v, own_v, own_two,
+    n, cots_ref, ctx_ref, wqkv_ref, x_ref, gains_ref, middle_cot_ref, feed_ref, table_ref, normed_any, mixed_any,
+    grad_ref, gain_out, table_out, input_ref,
+    normed_v, mixed_v, own_v,
     give, got, over, came, sc_send, sc_recv,
-    give_two, got_two, over_two, came_two, sd_send, sd_recv,
     put, inbox, ring_send, ring_recv,
     tables, pieces_v, spare_v, sum_v, last_v,
     t_send, t_recv, g_send, g_recv, h_send, h_recv, load_sem,
 ):
     place = Place(n)
-    size = x_ref.shape[0]
+    size, features = x_ref.shape
     load_n = pltpu.make_async_copy(normed_any, normed_v, load_sem.at[0])
     load_m = pltpu.make_async_copy(mixed_any, mixed_v, load_sem.at[1])
-    load_d = pltpu.make_async_copy(wdown_any, down_v, load_sem.at[2])
-    for copy in (load_n, load_m, load_d):
-        copy.start()
+    load_n.start()
+    load_m.start()
     place.barrier(everyone=True)
 
     def peer(k):
@@ -941,40 +1105,26 @@
     for copy in table_copies:
         copy.start()
     scatter = PairScatter(place, give, got, over, came, sc_send, sc_recv)
-    downs = PairScatter(place, give_two, got_two, over_two, came_two, sd_send, sd_recv)
 
     def term(slot):
-        left = matmul_tn(slot_columns(normed_v, slot, n), cots_ref[...])
+        left = matmul(normed_v[slot], cots_ref[...])
         return jnp.concatenate([left, matmul_tn(slot_columns(mixed_v, slot, n), ctx_ref[...])], axis=1)
 
-    ring = RingScatter(place, term, grad_ref, put, inbox, ring_send, ring_recv)
-
-    def both(step):
-        for way in (0, 1):
-            ring.advance(way, step)
+    ring = RingScatter(place, term, put, inbox, ring_send, ring_recv)
 
     def part(owner):
-        weight = wqkv_ref[...].reshape(-1, wqkv_ref.shape[2])
-        return matmul_nt(cots_ref[block_rows(place, owner, size), :], weight)
-
-    def part_two(owner):
-        weight = down_v[...].reshape(-1, down_v.shape[2])
-        return matmul_nt(hidden_ref[block_rows(place, owner, size), :], weight)
+        return matmul_nt(cots_ref[block_rows(owner, size), :], flat(wqkv_ref))
 
     scatter.far(part(place.far))
-    scatter.twin(part(place.twin))
     load_n.wait()
     load_m.wait()
-    both(0)
+    ring.advance(0)
+    scatter.twin(part(place.twin))
     scatter.mate(part(place.mate))
+    ring.advance(1)
     own_v[...] = part(place.m)
-    load_d.wait()
-    downs.far(part_two(place.far))
-    downs.twin(part_two(place.twin))
-    both(1)
-    downs.mate(part_two(place.mate))
-    own_two[...] = part_two(place.m)
-    both(2)
+    spread = gain_spread(n, features)
+    ring.advance(2)
     chunk_rows = size // 2
     gain = gains_ref[0:1, :]
     total = jnp.zeros_like(gain)
@@ -984,16 +1134,14 @@
         through, terms = norm_back(x_ref[rows, :], gain, grad)
         input_ref[rows, :] = middle_cot_ref[rows, :] + through
         total += jnp.sum(terms, axis=0, keepdims=True)
-    inside, kind = gain_lanes(n, (n * 4 * 8, gain.shape[1]))
+    inside, kind = gain_lanes(n, (n * 4 * 8, features))
     rows = jnp.where(inside & (kind == 0), total, 0.0) + jnp.where(inside & (kind == 1), feed_ref[0:1, :], 0.0)
-    rows = lax.dot_general(
-        rows, spread_ref[...].astype(F32), (((1,), (1,)), ((), ())), precision=lax.Precision.HIGHEST, preferred_element_type=F32
-    )
+    rows = lax.dot_general(rows, spread, (((1,), (1,)), ((), ())), precision=HIGHEST, preferred_element_type=F32)
     pieces_v[...] = rows.reshape(pieces_v.shape)
     around = [remote(pieces_v.at[lax.rem(place.d + k, n)], spare_v.at[n - k], g_send.at[k], g_recv.at[k], peer(k)) for k in range(1, n)]
     for copy in around:
         copy.start()
-    both(3)
+    ring.advance(3)
     table = table_ref[...]
     for k in range(1, n):
         remote(table_ref, tables.at[n - k], t_send.at[k], t_recv.at[k], peer(k)).wait_recv()
@@ -1009,45 +1157,39 @@
         target = lax.rem(place.m + k, 4)
         last.append(remote(sum_v.at[target], last_v.at[4 - k], h_send.at[k], h_recv.at[k], {"mp": target}))
         last[-1].start()
-    for chunk in range(2):
-        rows = slice(chunk * chunk_rows, (chunk + 1) * chunk_rows)
-        output_ref[rows, :] = middle_ref[rows, :] + downs.take(chunk, own_two[rows, :])
-    ring.finish()
+    grad_ref[...] = ring.total()
     sums = sum_v[place.m]
     for k in range(1, 4):
         remote(sum_v.at[0], last_v.at[4 - k], h_send.at[k], h_recv.at[k], {"mp": place.mate}).wait_recv()
         sums += last_v[4 - k]
     gain_out[...] = sums
+    ring.finish()
     scatter.finish()
-    downs.finish()
     for copy in table_copies + around + last:
         copy.wait_send()
 
 
-def leave_part(n, cots, ctx, wqkv, x, gains, middle_cot, feed, table, spread, middle, hidden, normed, mixed, wdown):
+def leave_part(n, cots, ctx, wqkv, x, gains, middle_cot, feed, table, normed, mixed):
     size, features = x.shape
     length, width = cots.shape
     rows = wqkv.shape[1]
     columns = width + ctx.shape[1]
+    shape = jax.ShapeDtypeStruct
     return pl.pallas_call(
         functools.partial(leave_kernel, n),
         name="leave",
         out_shape=(
-            jax.ShapeDtypeStruct((rows, columns), F32),
-            jax.ShapeDtypeStruct((8, 128), F32),
-            jax.ShapeDtypeStruct((8, 128), F32),
-            jax.ShapeDtypeStruct((size, features), F32),
-            jax.ShapeDtypeStruct((size, features), F32),
+            shape((rows, columns), F32),
+            shape((8, 128), F32),
+            shape((8, 128), F32),
+            shape((size, features), F32),
         ),
-        in_specs=[VMEM_SPEC] * 11 + [ANY_SPEC] * 3,
-        out_specs=(VMEM_SPEC,) * 5,
+        in_specs=[VMEM_SPEC] * 8 + [ANY_SPEC] * 2,
+        out_specs=(VMEM_SPEC,) * 4,
         scratch_shapes=[
+            pltpu.VMEM(normed.shape, BF16),
             pltpu.VMEM((length, features), BF16),
-            pltpu.VMEM((length, features), BF16),
-            pltpu.VMEM(wdown.shape, BF16),
             pltpu.VMEM((size, features), F32),
-            pltpu.VMEM((size, features), F32),
-            *PairScatter.scratch(size, features),
             *PairScatter.scratch(size, features),
             *RingScatter.scratch(n, rows, columns),
             pltpu.VMEM((n, 8, 128), F32),
@@ -1058,15 +1200,52 @@
             DMA((n,)), DMA((n,)),
             DMA((n,)), DMA((n,)),
             DMA((4,)), DMA((4,)),
-            DMA((3,)),
+            DMA((2,)),
         ],
         compiler_params=pltpu.CompilerParams(collective_id=3, has_side_effects=True),
-    )(cots, ctx, wqkv, x, gains, middle_cot, feed, table, spread, middle, hidden, normed, mixed, wdown)
-
-
-THRESHOLDS = (8, 12, 16, 23, 32, 46, 64, 91)
-HIGHEST = lax.Precision.HIGHEST
-MASKED = -1e30
+    )(cots, ctx, wqkv, x, gains, middle_cot, feed, table, normed, mixed)
+
+
+def finish_kernel(
+    own_ref, from_left_ref, from_right_ref, attention_ref, gain_ref, table_ref, output_in, input_in,
+    gate_out, lift_out, down_out, query_out, key_out, value_out, mixer_out, gain_out, gain_two_out, table_out, output_out, input_out,
+):
+    hidden = gate_out.shape[1]
+    heads = query_out.shape[1]
+    for k, out in enumerate((gate_out, lift_out, down_out)):
+        total = own_ref[k] + from_left_ref[k].astype(F32) + from_right_ref[k].astype(F32)
+        out[...] = total[:, :hidden]
+    for k, out in enumerate((query_out, key_out, value_out)):
+        out[...] = attention_ref[...][:, k * heads : (k + 1) * heads]
+    mixer_out[...] = attention_ref[...][:, 3 * heads :].T
+    per = gain_out.shape[0]
+    gain_out[...] = gain_ref[0:1, :per].reshape(per)
+    gain_two_out[...] = gain_ref[1:2, :per].reshape(per)
+    table_out[...] = table_ref[...][: table_out.shape[0], : table_out.shape[1]]
+    output_out[...] = output_in[...]
+    input_out[...] = input_in[...]
+
+
+def finish(own, from_left, from_right, attention, gain, table, output, input_grad, hidden, heads, count, buckets, per):
+    rows = own.shape[1]
+    shape = jax.ShapeDtypeStruct
+    square = shape((rows, heads), F32)
+    return pl.pallas_call(
+        finish_kernel,
+        name="finish",
+        out_shape=(
+            *(shape((rows, hidden), F32),) * 3,
+            square, square, square,
+            shape((heads, rows), F32),
+            shape((per,), F32),
+            shape((per,), F32),
+            shape((count, buckets), F32),
+            shape(output.shape, F32),
+            shape(input_grad.shape, F32),
+        ),
+        in_specs=[VMEM_SPEC] * 8,
+        out_specs=(VMEM_SPEC,) * 12,
+    )(own, from_left, from_right, attention, gain, table, output, input_grad)
 
 
 def bucket_table(length):
@@ -1326,19 +1505,14 @@
     )
 
 
-BLOCK = 256
-KINDS = 5
-
-
-def tile_buckets(block):
-    column = jnp.arange(2 * block)
-    column = jnp.where(column < block, column, column - 2 * block)
-    kind = jnp.arange(KINDS)[:, None]
-    offset = column[None, :] + (kind - 2) * block
-    offset = jnp.where(kind == 0, -2 * block, jnp.where(kind == KINDS - 1, 2 * block, offset))
-    distance = jnp.abs(offset)
-    far_bucket = 7 + sum(((distance >= limit).astype(jnp.int32) for limit in THRESHOLDS))
-    return jnp.where(distance < 8, distance, far_bucket) + jnp.where(offset > 0, 16, 0)
+def ring_order(n):
+    return [2 * p if p < n // 2 else 2 * (n - 1 - p) + 1 for p in range(n)]
+
+
+def to_neighbours(n, right, left):
+    ring = ring_order(n)
+    onward = [(ring[p], ring[(p + 1) % n]) for p in range(n)]
+    return lax.ppermute(right, "dp", onward), lax.ppermute(left, "dp", [(b, a) for a, b in onward])
 
 
 def fused(
@@ -1358,61 +1532,54 @@
     cotangent,
 ):
     x, cot = inputs[0], cotangent[0]
-    size = x.shape[0]
-    hidden_here = w_gate.shape[1]
-    heads = rel_table.shape[1]
-    head_width = w_query.shape[1]
-    per = attend_gain.shape[0]
-    spare = -hidden_here % 128
-    gain = jnp.pad(jnp.stack([attend_gain, feed_gain]), ((0, 6), (0, 128 - per)))
-    spread_rows = (jnp.arange(x.shape[1])[None, :] % per == jnp.arange(128)[:, None]).astype(BF16)
-    attention = jnp.concatenate([w_query, w_key, w_value, w_mixer.T], axis=1).astype(BF16)
-    wgate, wlift, wdown = (
-        jnp.pad(part.astype(BF16), ((0, 0), (0, spare))) for part in (w_gate, w_lift, w_down.T)
-    )
-    onehot = (tile_buckets(BLOCK)[..., None] == jnp.arange(128)).astype(F32)
-    count = rel_table.shape[0]
-    lines = jnp.einsum("tkb,bh->htk", onehot[..., :count], rel_table, precision=HIGHEST)
-    lines = jnp.pad(lines.reshape(heads * KINDS, -1), ((0, 1), (0, 0)))
-
-    normed, cots, gate_full, qkv, wqkv, wmix, gains, tiles = enter(
-        n, x, cot, gain, spread_rows, attention, wgate, lines
-    )
+    normed, cots, gate_full, qkv, wqkv, wmix, tiles, lift, down, gains = enter(
+        n, x, cot, attend_gain, feed_gain, w_query, w_key, w_value, w_mixer, w_gate, w_lift, w_down.T, rel_table.T
+    )
+    from_left, from_right = to_neighbours(n, lift, lift)
     context, context32, logsum = attend(qkv, segments, tiles)
     second, lift_full, down_full, bend, slope, hidden, middle = middle_part(
-        n, context, wmix, x, gains, wlift, wdown, gate_full
-    )
-    mixed, middle_cot, feed, down_term, gate_term, lift_term = back_part(
+        n, context, wmix, x, gains, lift, from_left, from_right, down, gate_full
+    )
+    mixed, pending, output, middle_cot, feed, own = back_part(
         n, middle, cot, gains, hidden, cots, second, bend, slope, gate_full, lift_full, down_full
     )
-    qkv_cot, table = attend_back(qkv, segments, tiles, context32, logsum, mixed, wmix, onehot)
-    attention_term, gain_term, table_term, input_grad, output = leave_part(
-        n, qkv_cot, context, wqkv, x, gains, middle_cot, feed, table, spread_rows, middle, hidden, normed, mixed, down_full
+    sums_left, sums_right = to_neighbours(n, pending[0], pending[1])
+    qkv_cot, table = attend_back(qkv, segments, tiles, context32, logsum, mixed, wmix)
+    attention_term, gain_term, table_term, input_grad = leave_part(
+        n, qkv_cot, context, wqkv, x, gains, middle_cot, feed, table, normed, mixed
+    )
+    gate_grad, lift_grad, down_grad, query_grad, key_grad, value_grad, mixer_grad, first, second, table_grad, output, input_grad = finish(
+        own, sums_left, sums_right, attention_term, gain_term, table_term, output, input_grad,
+        w_gate.shape[1], w_query.shape[1], rel_table.shape[1], rel_table.shape[0], attend_gain.shape[0],
     )
     return (
         output[None],
         input_grad[None],
-        gain_term[0, :per],
-        gain_term[1, :per],
-        attention_term[:, :head_width],
-        attention_term[:, head_width : 2 * head_width],
-        attention_term[:, 2 * head_width : 3 * head_width],
-        attention_term[:, 3 * head_width :].T,
-        table_term[:heads, :count].T,
-        gate_term[:, :hidden_here],
-        lift_term[:, :hidden_here],
-        down_term[:, :hidden_here].T,
-    )
-
-
-def kernels_fit(mesh):
-    return mesh.shape["dp"] == 8 and mesh.shape["mp"] == 4
+        first,
+        second,
+        query_grad,
+        key_grad,
+        value_grad,
+        mixer_grad,
+        table_grad.T,
+        gate_grad,
+        lift_grad,
+        down_grad.T,
+    )
+
+
+def layer(mesh, inputs, *rest):
+    n, pairs = mesh.shape["dp"], mesh.shape["mp"]
+    tokens, hidden = inputs.shape[1] * pairs, rest[8].shape[1]
+    slots = inputs.shape[2] // n
+    if n == 8 and pairs == 4 and slots % 64 == 0 and hidden + -hidden % 128 == tokens and tokens % BLOCK == 0:
+        return fused(n, inputs, *rest)
+    return native(inputs, *rest)
 
 
 def solution(mesh):
-    local = functools.partial(fused, mesh.shape["dp"]) if kernels_fit(mesh) else native
     return jax.shard_map(
-        local,
+        functools.partial(layer, mesh),
         mesh=mesh,
         in_specs=(
             P("dp", "mp", None),

time: 392 us -> 316 us (0.81)
  Pallas kernels: 364 us -> 301 us
  local copies, waits for them, and re-layouts: 16.2 us -> 5.19 us
  other arithmetic: 7.45 us -> 0 us
  starting transfers between devices: 0 us -> 4.26 us
    pallas_call x1, Pallas kernels: 104 us -> 80.4 us  [back_part(): pl.pallas_call(functools.partial(back_kernel, n), name='back', out_shape=...]
    pallas_call x1, Pallas kernels: 46.1 us -> 25.7 us  [attend_back(): pl.pallas_call(attend_back_kernel, name='attend_back', out_shape=(jax.Sha...]
    pallas_call x1, Pallas kernels: 82.2 us -> 63.2 us  [middle_part(): pl.pallas_call(functools.partial(middle_kernel, n), name='middle', out_sh...]
    pallas_call x1, Pallas kernels: 49 us -> 41.2 us  [leave_part(): pl.pallas_call(functools.partial(leave_kernel, n), name='leave', out_shap...]
    pallas_call x0 -> x1, Pallas kernels: none -> 6.46 us  [finish(): pl.pallas_call(finish_kernel, name='finish', out_shape=(*(shape((rows, hi...]
    unnamed x28 -> x8, local copies, waits for them, and re-layouts: 7.81 us -> 2.25 us
    ppermute x0 -> x4, starting transfers between devices: none -> 4.26 us  [the longest x2 2.32 us: to_neighbours(): lax.ppermute(left, 'dp', [(b, a) for a, b in onward])]
    another operation x4 -> x0, other arithmetic: 4.16 us -> none
  transfers between devices with their start and end apart: 0 -> 4, of which waited for: 0 -> 0; matrix products, arithmetic and copies ran while one was open for 0% -> 0% of each run, Pallas kernels for 0% -> 25%
where the time goes in v2:
time: 316 us; the launch traced here: 312 us
  Pallas kernels  301 us (95%)
  local copies, waits for them, and re-layouts  5.19 us (2%)
  starting transfers between devices  4.26 us (1%)
    pallas_call x1, Pallas kernels, back_part(): pl.pallas_call(functools.partial(back_kernel, n), name='back', out_shape=...  80.4 us
    pallas_call x1, Pallas kernels, enter(): pl.pallas_call(functools.partial(enter_kernel, n), name='enter', out_shap...  72.6 us
    pallas_call x1, Pallas kernels, middle_part(): pl.pallas_call(functools.partial(middle_kernel, n), name='middle', out_sh...  63.2 us
    pallas_call x1, Pallas kernels, leave_part(): pl.pallas_call(functools.partial(leave_kernel, n), name='leave', out_shap...  41.2 us
    pallas_call x1, Pallas kernels, attend_back(): pl.pallas_call(attend_back_kernel, name='attend_back', out_shape=(jax.Sha...  25.7 us
    pallas_call x1, Pallas kernels, attend(): pl.pallas_call(attend_kernel, name='attend', out_shape=(jax.ShapeDtypeStr...  11.8 us
    pallas_call x1, Pallas kernels, finish(): pl.pallas_call(finish_kernel, name='finish', out_shape=(*(shape((rows, hi...  6.46 us
  transfers between devices with their start and end apart: 4, of which 0 were waited for; matrix products, arithmetic and copies ran while one was open for 0% of the time, Pallas kernels for 25%

profile of v2, /device:TPU:0, one launch (start us, length us, event | category | flops | bytes accessed | tf_op | source)
XLA Modules:
  0.0 311.8 jit_solution(6000252288468315334)
XLA Ops:
  0.6 72.6 %enter.1 = (bf16[8,192,1024]{2,1,0:T(8,128)(2,1)}, bf16[8,192,1024]{2,1,0:T(8,128)(2,1)}, bf16[8,192,1024]{2,1,0:T(8,128)(2,1)}, bf16[1024,576]{1,0:T(8,128)(2,1...) custom-call(f32[256,1536]{1,0:T(8,128)} %bitcast.12, ...), custom_call_target="tpu_custom_call" | custom-call | tf_op jit(solution)/shard_map/enter/pallas_call | solution.py:692
  73.3 1.2 collective-permute-start.1
  74.4 1.1 collective-permute-start
  75.5 11.8 %attend.1 = (bf16[1024,192]{1,0:T(8,128)(2,1)}, f32[1024,192]{1,0:T(8,128)}, f32[1024,8]{1,0:T(8,128)}) custom-call(s32[1,1024]{1,0:T(1,128)} %segr_ref.3, bf16[1024,576]{1,0:T(8,128)(2,1)} %get-tuple-element.56.qkv_ref, s32[1,1024]{1,0:T(1,128)} %segr_ref.3, f32[3,5,256,256]{3,2,1,0:T(8,128)} %get-tuple-element.57.tiles_ref), custom_call_target="tpu_custom_call" | custom-call | flops 1207959552 | bytes 8388608 | tf_op jit(solution)/shard_map/attend/pallas_call | solution.py:380
  87.4 0.0 collective-permute-done.1.from_right_ref
  87.4 0.0 copy-start.2
  87.4 0.0 collective-permute-done.from_left_ref
  87.4 0.0 copy-start.3
  87.4 0.7 copy-done.2
  88.1 0.1 copy-done.3
  88.2 63.2 %middle.1 = (bf16[8,192,1024]{2,1,0:T(8,128)(2,1)}, bf16[8,192,1024]{2,1,0:T(8,128)(2,1)}, bf16[8,192,1024]{2,1,0:T(8,128)(2,1)}, f32[1024,1024]{1,0:T(8,128)}, ...) custom-call(bf16[1024,192]{1,0:T(8,128)(2,1)} %get-tuple-element.58.ctx_ref, ...), custom_call_target="tpu_custom_call" | custom-call | tf_op jit(solution)/shard_map/middle/pallas_call | solution.py:838
  151.4 80.4 %back.1 = (bf16[1024,1536]{1,0:T(8,128)(2,1)}, bf16[2,3,192,1024]{3,2,1,0:T(8,128)(2,1)}, f32[256,1536]{1,0:T(8,128)}, f32[256,1536]{1,0:T(8,128)}, f32[8,1536]{1,0:T(8,128)}, /*index=5*/f32[3,192,1024]{2,1,0:T(8,128)}) custom-call(f32[256,1536]{1,0:T(8,128)} %get-tuple-element.64.middle_ref, f32[8,1536]{1,0:T(8,128)} %get-tuple-element.60.gains_ref, ...), custom_call_target="tpu_custom_call" | custom-call | tf_op jit(solution)/shard_map/back/pallas_call | solution.py:1048
  231.8 2.9 slice_bitcast_fusion
  234.7 1.2 collective-permute-start.3
  235.9 0.9 collective-permute-start.2
  236.7 25.7 %attend_back.1 = (bf16[1024,576]{1,0:T(8,128)(2,1)}, f32[8,128]{1,0:T(8,128)}) custom-call(s32[1,1024]{1,0:T(1,128)} %segr_ref.3, bf16[1024,576]{1,0:T(8,128)(2,1)} %get-tuple-element.56.qkv_ref, s32[1,1024]{1,0:T(1,128)} %segr_ref.3, f32[3,5,256,256]{3,2,1,0:T(8,128)} %get-tuple-element.57.tiles_ref, f32[1024,192]{1,0:T(8,128)} %get-tuple-element.74.ctx32_ref, ...), custom_call_target="tpu_custom_call" | custom-call | flops 4831838208 | bytes 33554432 | tf_op jit(solution)/shard_map/attend_back/pallas_call | solution.py:488
  262.5 41.2 %leave.1 = (f32[192,768]{1,0:T(8,128)}, f32[8,128]{1,0:T(8,128)}, f32[8,128]{1,0:T(8,128)}, f32[256,1536]{1,0:T(8,128)}) custom-call(bf16[1024,576]{1,0:T(8,128)(2,1)} %get-tuple-element.77.cots_ref, bf16[1024,192]{1,0:T(8,128)(2,1)} %get-tuple-element.58.ctx_ref, bf16[8,192,576]{2,1,0:T(8,128)(2,1)} %get-tuple-element.78.wqkv_ref, f32[256,1536]{1,0:T(8,128)} %bitcast.14, ...), custom_call_target="tpu_custom_call" | custom-call | tf_op jit(solution)/shard_map/leave/pallas_call | solution.py:1178
  303.7 0.0 collective-permute-done.3.from_right_ref
  303.7 0.0 copy-start
  303.7 0.0 collective-permute-done.2.from_left_ref
  303.7 0.0 copy-start.1
  303.7 1.0 copy-done
  304.7 0.4 copy-done.1
  305.1 6.5 %finish.1 = (f32[192,992]{1,0:T(8,128)}, f32[192,992]{1,0:T(8,128)}, f32[192,992]{1,0:T(8,128)}, f32[192,192]{1,0:T(8,128)}, f32[192,192]{1,0:T(8,128)}, /*index...) custom-call(f32[3,192,1024]{2,1,0:T(8,128)} %get-tuple-element.72.ow, ...), custom_call_target="tpu_custom_call" | custom-call | tf_op jit(solution)/shard_map/finish/pallas_call | solution.py:1233
Async XLA Ops:
  73.3 14.1 %collective-permute-start.1 = (bf16[192,1024]{1,0:T(8,128)(2,1)}, bf16[192,1024]{1,0:T(8,128)(2,1)S(1)}, u32[]{:S(2)}, u32[]{:S(2)}) collective-permute-start(bf16[192,1024]{1,0:T(8,128)(2,1)} %get-tuple-element.61.lift_ref), channel_id=1, source_target_pairs={{8,0},{16,8},{24,16},{28,24},{20,28},{12,20},{4,12},{0,4},{9,1},{1... | collective-permute-start | bytes 1179656 | tf_op jit(solution)/shard_map/ppermute | solution.py:1515
  74.4 12.9 %collective-permute-start = (bf16[192,1024]{1,0:T(8,128)(2,1)}, bf16[192,1024]{1,0:T(8,128)(2,1)S(1)}, u32[]{:S(2)}, u32[]{:S(2)}) collective-permute-start(bf16[192,1024]{1,0:T(8,128)(2,1)} %get-tuple-element.61.lift_ref), channel_id=1, source_target_pairs={{0,8},{8,16},{16,24},{24,28},{28,20},{20,12},{12,4},{4,0},{1,9},{9... | collective-permute-start | bytes 1179656 | tf_op jit(solution)/shard_map/ppermute | solution.py:1515
  87.4 0.7 copy-start.2
  87.4 0.9 copy-start.3
  234.7 69.0 %collective-permute-start.3 = (bf16[3,192,1024]{2,1,0:T(8,128)(2,1)}, bf16[3,192,1024]{2,1,0:T(8,128)(2,1)S(1)}, u32[]{:S(2)}, u32[]{:S(2)}) collective-permute-start(bf16[3,192,1024]{2,1,0:T(8,128)(2,1)} %get-tuple-element.100), channel_id=1, source_target_pairs={{8,0},{16,8},{24,16},{28,24},{20,28},{12,20},{4,12},{0,4},{9,1},{1... | collective-permute-start | bytes 3538952 | tf_op jit(solution)/shard_map/ppermute | solution.py:1515
  235.9 67.8 %collective-permute-start.2 = (bf16[3,192,1024]{2,1,0:T(8,128)(2,1)S(1)}, bf16[3,192,1024]{2,1,0:T(8,128)(2,1)S(1)}, u32[]{:S(2)}, u32[]{:S(2)}) collective-permute-start(bf16[3,192,1024]{2,1,0:T(8,128)(2,1)S(1)} %get-tuple-element.101), channel_id=1, source_target_pairs={{0,8},{8,16},{16,24},{24,28},{28,20},{20,12},{12,4},{4,0},{1,9},{9... | collective-permute-start | bytes 3538952 | tf_op jit(solution)/shard_map/ppermute | solution.py:1515
  303.7 1.0 copy-start
  303.7 1.4 copy-start.1
